TPU v7x, 256 devices: a whole 4x4x8 slice. The times are simulated.
256 devices in a mesh: rows: 64 (over z, y, core), sub: 4 (over x).
Axes of the slice: x: 4, y: 4, z: 8, core: 2. Of those that a mesh axis runs over, the one named last changes fastest.
Arguments:
- stiffness_tiles: bfloat16 [64, 4, 128, 128, 128], P('rows', 'sub'), may hold values from -0.5 to 0.5
- damping_tiles: bfloat16 [64, 4, 128, 128, 128], P('rows', 'sub'), may hold values from -0.5 to 0.5
- tile_map: int32 [64, 4, 2, 128], P('rows', 'sub'), may hold values from -1 to 767, as said below
- inv_mass: float32 [2097152], P(('rows', 'sub')), may hold values from 0.5 to 2
- spectral_shift: float32 [], replicated, may hold values from 0.5 to 1.5
- basis: float32 [58, 2097152], P(None, ('rows', 'sub')), may hold values from -20 to 20
- compact: float32 [2, 58, 57], replicated, may hold values from -0.54 to 0.54
Outputs:
- new_basis: float32 [2, 2097152], P(None, ('rows', 'sub'))
- compact_out: float32 [2, 60, 59], replicated
- hessenberg: float32 [59, 2], replicated
Inputs may be any that keep to these rules, and one draw needn't show every extreme that they name: tile_map[r, s, 0, t] is the tile row of part r that slot t adds to, or -1 for an unused slot; the used slots of a device come first, and some device uses all 128. tile_map[r, s, 1, t] is the source column tile counted from the start of part r - 1.
All inputs are finite; a program needn't handle non-finite values.
Results may differ from a plain program's by a relative error of at most 0.0033.
Values may be sent and summed in bfloat16 or wider, within the bound.
A program may use at most 64 MiB of HBM per device.

v0:
```python
import jax
import jax.numpy as jnp
from jax import lax
from jax.sharding import Mesh
from jax.sharding import PartitionSpec as P

ITERS = 2
ROWS = ("rows_0", "rows_1", "rows_2")
ROWS_SUB = ("rows_0", "rows_1", "rows_2", "sub")


precise = lax.Precision.HIGHEST


def padded(array, sides, width):
    for axis, dim in sides:
        devices, length = (lax.axis_size(axis), array.shape[dim])
        up = [(i, (i + 1) % devices) for i in range(devices - 1)]
        down = [(j, i) for i, j in up]
        last = lax.slice_in_dim(array, length - width, length, axis=dim)
        initial = lax.slice_in_dim(array, 0, width, axis=dim)
        before = lax.ppermute(last, axis, up)
        after = lax.ppermute(initial, axis, down)
        array = jnp.concatenate([before, array, after], axis=dim)
    return array


def joined_along(blocks, dim):
    dims = list(blocks.shape[1:])
    dims[dim] *= blocks.shape[0]
    return jnp.moveaxis(blocks, 0, dim).reshape(dims)


def from_everyone(array, axis):
    copies = jnp.broadcast_to(array, (lax.axis_size(axis), *array.shape))
    return lax.all_to_all(copies, axis, split_axis=0, concat_axis=0, tiled=True)


def collect(array, axis, dim):
    return joined_along(from_everyone(array, axis), dim)


def in_blocks(array, dim, devices):
    dims = array.shape
    blocks = array.reshape(*dims[:dim], devices, dims[dim] // devices, *dims[dim + 1 :])
    return jnp.moveaxis(blocks, dim, 0)


def sent_and_summed(array, axis, dim):
    blocks = in_blocks(array, dim, lax.axis_size(axis))
    arrived = lax.all_to_all(blocks, axis, split_axis=0, concat_axis=0, tiled=True)
    return arrived.sum(axis=0)


def taken_together(array, axis):
    everything = from_everyone(array, axis)
    return jnp.sum(everything, axis=0)


def over_axes(array, axes):
    far, near = axes
    return taken_together(taken_together(array, near), far)


def in_one(arrays, axis):
    line, at, done = (jnp.concatenate([a.reshape(-1) for a in arrays]), 0, [])
    total = over_axes(line, axis)
    for a in arrays:
        done.append(total[at : at + a.size].reshape(a.shape))
        at += a.size
    return tuple(done)


def compact_update(upper_half, lower_half, coefficients, norm_value, lower_tail):
    columns = upper_half.shape[1]
    zero_row = jnp.zeros((1, columns), upper_half.dtype)
    upper_ext = jnp.concatenate([upper_half, zero_row], 0)
    lower_ext = jnp.concatenate([lower_half, zero_row], 0)
    upper_coeffs = jnp.concatenate([coefficients, norm_value[None]])
    lower_coeffs = jnp.concatenate([lower_tail, jnp.zeros((1,), lower_tail.dtype)])
    weights = jnp.zeros((columns,), upper_half.dtype)
    for repeat_index in range(2):
        projection = jnp.dot(upper_coeffs, upper_ext, precision=precise) + jnp.dot(
            lower_coeffs, lower_ext, precision=precise
        )
        upper_coeffs = upper_coeffs - jnp.dot(upper_ext, projection, precision=precise)
        lower_coeffs = lower_coeffs - jnp.dot(lower_ext, projection, precision=precise)
        weights = weights + projection
    beta_norm = jnp.sqrt(
        jnp.sum(upper_coeffs * upper_coeffs) + jnp.sum(lower_coeffs * lower_coeffs) + 1e-06
    )
    upper_new = jnp.concatenate([upper_ext, (upper_coeffs / beta_norm)[:, None]], 1)
    lower_new = jnp.concatenate([lower_ext, (lower_coeffs / beta_norm)[:, None]], 1)
    return (upper_new, lower_new, weights, beta_norm)


def tile_products(damping, stiffness, target, source, blocked, tile_rows):
    picked_damp = blocked[0][source]
    picked_stiff = blocked[1][source]
    product = jnp.einsum("sij,sj->si", damping, picked_damp, preferred_element_type=jnp.float32)
    product = product + jnp.einsum(
        "sij,sj->si", stiffness, picked_stiff, preferred_element_type=jnp.float32
    )
    selector = (target[None, :] == jnp.arange(tile_rows, dtype=jnp.int32)[:, None]).astype(
        jnp.float32
    )
    return jnp.dot(selector, product, precision=precise)


def on_device(stiffness_tiles, damping_tiles, tile_map, inv_mass, spectral_shift, basis, compact):
    rows_count = lax.axis_size(ROWS)
    sub_count = lax.axis_size("sub")
    tile_size = stiffness_tiles.shape[-1]
    local_rows = basis.shape[1]
    part_rows = sub_count * local_rows
    tile_rows = part_rows // tile_size
    unknowns = local_rows * rows_count * sub_count
    target = tile_map[0, 0, 0]
    source = tile_map[0, 0, 1]
    damping = damping_tiles[0, 0]
    stiffness = stiffness_tiles[0, 0]
    held = basis
    upper_half = compact[0]
    lower_half = compact[1]
    new_columns = []
    hess_columns = []
    for iteration in range(ITERS):
        upper_last = upper_half[:, -1]
        lower_last = lower_half[:, -1]
        upper_vec = jnp.dot(upper_last, held, precision=precise)
        lower_vec = jnp.dot(lower_last, held, precision=precise)
        vectors = jnp.stack([upper_vec, lower_vec]).astype(jnp.bfloat16)
        beside = padded(vectors, ((ROWS, 1),), local_rows)
        spread = collect(beside.reshape(2, 3, 1, local_rows), "sub", 2)
        window = spread.reshape(2, 3 * part_rows)
        blocked = window.reshape(2, 3 * tile_rows, tile_size)
        summed = tile_products(damping, stiffness, target, source, blocked, tile_rows)
        partial_value = summed.reshape(-1)
        coupled = sent_and_summed(partial_value, "sub", 0)
        image = spectral_shift * upper_vec - inv_mass * coupled
        image_inner, image_self, gram = in_one(
            (
                jnp.dot(held, image, precision=precise),
                jnp.sum(image * image),
                jnp.dot(held, held.T, precision=precise),
            ),
            ("rows_0", ("rows_1", "rows_2", "sub")),
        )
        first_part = image_inner / unknowns
        gram = gram / unknowns
        second_part = first_part - jnp.dot(gram, first_part, precision=precise)
        coefficients = first_part + second_part
        residual_two = image - jnp.dot(coefficients, held, precision=precise)
        square_mean = (
            image_self / unknowns
            - 2.0 * jnp.dot(coefficients, first_part, precision=precise)
            + jnp.dot(
                coefficients, jnp.dot(gram, coefficients, precision=precise), precision=precise
            )
        )
        norm_value = jnp.sqrt(square_mean + 1e-06)
        column = residual_two / norm_value
        lower_tail = upper_last + spectral_shift * lower_last
        upper_half, lower_half, weights, beta_norm = compact_update(
            upper_half, lower_half, coefficients, norm_value, lower_tail
        )
        held = jnp.concatenate([held, column[None]], 0)
        new_columns.append(column)
        hess_columns.append(
            jnp.concatenate(
                [weights, beta_norm[None], jnp.zeros((ITERS - 1 - iteration,), weights.dtype)]
            )
        )
    return (
        jnp.stack(new_columns),
        jnp.stack([upper_half, lower_half]),
        jnp.stack(hess_columns, axis=1),
    )


def solution(mesh):
    split = Mesh(
        mesh.devices.reshape(8, 4, 2, mesh.shape["sub"]), ("rows_0", "rows_1", "rows_2", "sub")
    )
    in_specs = (
        P(ROWS, "sub", None, None, None),
        P(ROWS, "sub", None, None, None),
        P(ROWS, "sub", None, None),
        P(ROWS_SUB),
        P(),
        P(None, ROWS_SUB),
        P(),
    )
    out_specs = (P(None, ROWS_SUB), P(), P())
    return jax.shard_map(
        on_device, mesh=split, in_specs=in_specs, out_specs=out_specs, check_vma=False
    )
```

profile of v0, /device:TPU:1, one launch (start us, length us, event | category | flops | bytes accessed | tf_op | source)
XLA Modules:
  0.0 183.8 jit_solution(13568724579908415418)
XLA Ops:
  0.6 1.1 fusion.90
  2.1 2.7 %fusion.46 = f32[1,8192]{1,0:T(1,128)S(1)} fusion(f32[58,8192]{1,0:T(8,128)} %param.12, f32[58]{0:T(128)S(1)} %get-tuple-element.51), kind=kOutput, calls=%fused_computation.106 | convolution fusion | flops 5701632 | bytes 1933544 | tf_op jit(solution)/shard_map/dot_general | solution.py:130
  4.8 1.1 fusion.44
  6.0 4.6 %collective-permute-start = (bf16[2,8192]{1,0:T(2,128)(2,1)S(1)}, bf16[2,8192]{1,0:T(2,128)(2,1)S(1)}, u32[]{:S(2)}, u32[]{:S(2)}) collective-permute-start(bf16[2,8192]{1,0:T(2,128)(2,1)S(1)} %pad_maximum_fusion.10), channel_id=1, source_target_pairs={{0,4},{4,8},{8,12},{12,16},{16,20},{20,24},{24,28},{28,32},{32,36}... | collective-permute-start | bytes 98312 | tf_op jit(solution)/shard_map/ppermute | solution.py:22
  10.6 1.9 %collective-permute-start.1 = (bf16[2,8192]{1,0:T(2,128)(2,1)S(1)}, bf16[2,8192]{1,0:T(2,128)(2,1)S(1)}, u32[]{:S(2)}, u32[]{:S(2)}) collective-permute-start(bf16[2,8192]{1,0:T(2,128)(2,1)S(1)} %pad_maximum_fusion.10), channel_id=1, source_target_pairs={{4,0},{8,4},{12,8},{16,12},{20,16},{24,20},{28,24},{32,28},{36,32}... | collective-permute-start | bytes 98312 | tf_op jit(solution)/shard_map/ppermute | solution.py:23
  12.6 3.3 %collective-permute-done.1 = bf16[2,8192]{1,0:T(2,128)(2,1)S(1)} collective-permute-done((bf16[2,8192]{1,0:T(2,128)(2,1)S(1)}, bf16[2,8192]{1,0:T(2,128)(2,1)S(1)}, u32[]{:S(2)}, u32[]{:S(2)}) %collective-permute-start.1) | collective-permute-done | bytes 32800 | tf_op jit(solution)/shard_map/ppermute | solution.py:23
  16.0 1.0 broadcast_in_dim.51
  17.0 4.0 %all-to-all-start = ((bf16[4,2,3,1,8192]{4,1,3,2,0:T(2,128)(2,1)}), bf16[4,2,3,1,8192]{4,1,3,2,0:T(2,128)(2,1)S(1)}, u32[]{:S(2)}, u32[]{:S(2)}) async-start(bf16[4,2,3,1,8192]{4,1,3,2,0:T(2,128)(2,1)} %broadcast_in_dim.51), calls=%async_computation | async-start | bytes 786432 | tf_op jit(solution)/shard_map/all_to_all | solution.py:36
  21.1 6.9 %all-to-all-done = bf16[4,2,3,1,8192]{4,1,3,2,0:T(2,128)(2,1)S(1)} async-done(((bf16[4,2,3,1,8192]{4,1,3,2,0:T(2,128)(2,1)}), bf16[4,2,3,1,8192]{4,1,3,2,0:T(2,128)(2,1)S(1)}, u32[]{:S(2)}, u32[]{:S(2)}) %all-to-all-start) | async-done | bytes 393248 | tf_op jit(solution)/shard_map/all_to_all | solution.py:36
  28.0 0.8 fusion.89
  29.8 0.7 gather_fusion
  30.5 0.7 gather_fusion.1
  31.2 4.6 %fusion.6 = f32[128,1,128]{2,1,0:T(1,128)S(1)} fusion(bf16[1,1,128,128,128]{4,3,2,1,0:T(8,128)(2,1)} %param.8, bf16[128,128,1]{1,0,2:T(8,128)(2,1)S(1)} %bitcast.296), kind=kOutput, calls=%fused_computation.10 | convolution fusion | flops 4194304 | bytes 4292608 | tf_op jit(solution)/shard_map/sij,sj->si/dot_general | solution.py:100
  35.8 2.3 %fusion.2 = f32[128,1,128]{2,1,0:T(1,128)S(1)} fusion(bf16[1,1,128,128,128]{4,3,2,1,0:T(8,128)(2,1)S(1)} %copy-done.1, bf16[128,128,1]{1,0,2:T(8,128)(2,1)S(1)} %bitcast.297), kind=kOutput, calls=%fused_computation.6 | convolution fusion | flops 4194304 | bytes 4292608 | tf_op jit(solution)/shard_map/sij,sj->si/dot_general | solution.py:101
  38.1 0.9 fusion.33
  38.9 3.3 %all-to-all-start.1 = ((f32[4,1,8192]{2,1,0:T(1,128)}), f32[4,1,8192]{2,1,0:T(1,128)S(1)}, u32[]{:S(2)}, u32[]{:S(2)}) async-start(f32[4,1,8192]{2,1,0:T(1,128)} %bitcast.17), calls=%async_computation.1 | async-start | bytes 262144 | tf_op jit(solution)/shard_map/all_to_all | solution.py:51
  42.3 1.8 fusion.101
  44.8 2.7 %all-to-all-done.1 = f32[4,1,8192]{2,1,0:T(1,128)S(1)} async-done(((f32[4,1,8192]{2,1,0:T(1,128)}), f32[4,1,8192]{2,1,0:T(1,128)S(1)}, u32[]{:S(2)}, u32[]{:S(2)}) %all-to-all-start.1) | async-done | bytes 131104 | tf_op jit(solution)/shard_map/all_to_all | solution.py:51
  47.7 0.6 multiply_reduce_fusion.1
  48.3 1.7 convolution_bitcast_fusion.21
  50.0 0.7 concatenate.58
  51.0 17.8 %all_to_all.52 = f32[32,1,3423]{2,1,0:T(1,128)S(1)} all-to-all(f32[32,1,3423]{2,1,0:T(1,128)S(1)} %broadcast_in_dim.52), channel_id=1, replica_groups=mesh['rows_0'=8,'rows_1'=4,'rows_2'=2,'sub'=4] {'rows_1','rows_2','sub'}, dimensions={0} | all-to-all | bytes 876288 | tf_op jit(solution)/shard_map/all_to_all | solution.py:36
  69.1 0.7 broadcast_in_dim.53
  69.8 8.2 %all-to-all-start.3 = ((f32[8,1,3423]{2,1,0:T(1,128)}), f32[8,1,3423]{2,1,0:T(1,128)S(1)}, u32[]{:S(2)}, u32[]{:S(2)}) async-start(f32[8,1,3423]{2,1,0:T(1,128)} %broadcast_in_dim.53), calls=%async_computation.3 | async-start | bytes 221184 | tf_op jit(solution)/shard_map/all_to_all | solution.py:36
  77.9 7.6 %all-to-all-done.3 = f32[8,1,3423]{2,1,0:T(1,128)S(1)} async-done(((f32[8,1,3423]{2,1,0:T(1,128)}), f32[8,1,3423]{2,1,0:T(1,128)S(1)}, u32[]{:S(2)}, u32[]{:S(2)}) %all-to-all-start.3) | async-done | bytes 109568 | tf_op jit(solution)/shard_map/all_to_all | solution.py:36
  85.7 0.6 slice.82
  86.4 0.8 multiply_reduce_fusion.3
  87.2 0.8 fusion.26
  91.0 0.8 multiply_reduce_fusion.6
  91.8 0.8 multiply_reduce_fusion.7
  92.5 1.1 fusion.68
  95.0 1.1 fusion.31
  96.2 1.1 fusion.30
  97.5 4.3 %collective-permute-start.2 = (bf16[2,8192]{1,0:T(2,128)(2,1)S(1)}, bf16[2,8192]{1,0:T(2,128)(2,1)S(1)}, u32[]{:S(2)}, u32[]{:S(2)}) collective-permute-start(bf16[2,8192]{1,0:T(2,128)(2,1)S(1)} %pad_maximum_fusion.11), channel_id=1, source_target_pairs={{0,4},{4,8},{8,12},{12,16},{16,20},{20,24},{24,28},{28,32},{32,36}... | collective-permute-start | bytes 98312 | tf_op jit(solution)/shard_map/ppermute | solution.py:22
  101.7 1.9 %collective-permute-start.3 = (bf16[2,8192]{1,0:T(2,128)(2,1)S(1)}, bf16[2,8192]{1,0:T(2,128)(2,1)S(1)}, u32[]{:S(2)}, u32[]{:S(2)}) collective-permute-start(bf16[2,8192]{1,0:T(2,128)(2,1)S(1)} %pad_maximum_fusion.11), channel_id=1, source_target_pairs={{4,0},{8,4},{12,8},{16,12},{20,16},{24,20},{28,24},{32,28},{36,32}... | collective-permute-start | bytes 98312 | tf_op jit(solution)/shard_map/ppermute | solution.py:23
  103.7 3.3 %collective-permute-done.3 = bf16[2,8192]{1,0:T(2,128)(2,1)S(1)} collective-permute-done((bf16[2,8192]{1,0:T(2,128)(2,1)S(1)}, bf16[2,8192]{1,0:T(2,128)(2,1)S(1)}, u32[]{:S(2)}, u32[]{:S(2)}) %collective-permute-start.3) | collective-permute-done | bytes 32800 | tf_op jit(solution)/shard_map/ppermute | solution.py:23
  107.4 9.1 %all_to_all.53 = bf16[4,2,3,1,8192]{4,1,3,2,0:T(2,128)(2,1)S(1)} all-to-all(bf16[4,2,3,1,8192]{4,1,3,2,0:T(2,128)(2,1)S(1)} %broadcast_in_dim.55), channel_id=1, replica_groups=mesh['rows_0'=8,'rows_1'=4,'rows_2'=2,'sub'=4] {'sub'}, dimensions={0} | all-to-all | bytes 786432 | tf_op jit(solution)/shard_map/all_to_all | solution.py:36
  116.5 0.8 fusion.88
  117.8 0.7 gather_fusion.3
  118.5 4.4 %fusion = f32[128,1,128]{2,1,0:T(1,128)S(1)} fusion(bf16[1,1,128,128,128]{4,3,2,1,0:T(8,128)(2,1)} %param.7, bf16[128,128,1]{1,0,2:T(8,128)(2,1)S(1)} %bitcast.299), kind=kOutput, calls=%fused_computation.4 | convolution fusion | flops 4194304 | bytes 4292608 | tf_op jit(solution)/shard_map/sij,sj->si/dot_general | solution.py:101
  123.4 0.7 gather_fusion.2
  124.1 4.4 %fusion.4 = f32[128,1,128]{2,1,0:T(1,128)S(1)} fusion(bf16[1,1,128,128,128]{4,3,2,1,0:T(8,128)(2,1)} %param.8, bf16[128,128,1]{1,0,2:T(8,128)(2,1)S(1)} %bitcast.298), kind=kOutput, calls=%fused_computation.8 | convolution fusion | flops 4194304 | bytes 4292608 | tf_op jit(solution)/shard_map/sij,sj->si/dot_general | solution.py:100
  128.6 0.9 fusion.32
  129.4 3.5 %all-to-all-start.5 = ((f32[4,1,8192]{2,1,0:T(1,128)}), f32[4,1,8192]{2,1,0:T(1,128)S(1)}, u32[]{:S(2)}, u32[]{:S(2)}) async-start(f32[4,1,8192]{2,1,0:T(1,128)} %bitcast.58), calls=%async_computation.5 | async-start | bytes 262144 | tf_op jit(solution)/shard_map/all_to_all | solution.py:51
  133.0 1.8 fusion.29
  134.9 2.9 %all-to-all-done.5 = f32[4,1,8192]{2,1,0:T(1,128)S(1)} async-done(((f32[4,1,8192]{2,1,0:T(1,128)}), f32[4,1,8192]{2,1,0:T(1,128)S(1)}, u32[]{:S(2)}, u32[]{:S(2)}) %all-to-all-start.5) | async-done | bytes 131104 | tf_op jit(solution)/shard_map/all_to_all | solution.py:51
  137.9 0.6 multiply_reduce_fusion
  138.5 1.7 convolution_bitcast_fusion.20
  140.2 0.7 concatenate.65
  141.0 1.0 broadcast_in_dim.56
  142.0 6.9 %all-to-all-start.6 = ((f32[32,1,3541]{2,1,0:T(1,128)}), f32[32,1,3541]{2,1,0:T(1,128)S(1)}, u32[]{:S(2)}, u32[]{:S(2)}) async-start(f32[32,1,3541]{2,1,0:T(1,128)} %broadcast_in_dim.56), calls=%async_computation.6 | async-start | bytes 917504 | tf_op jit(solution)/shard_map/all_to_all | solution.py:36
  149.2 10.5 %all-to-all-done.6 = f32[32,1,3541]{2,1,0:T(1,128)S(1)} async-done(((f32[32,1,3541]{2,1,0:T(1,128)}), f32[32,1,3541]{2,1,0:T(1,128)S(1)}, u32[]{:S(2)}, u32[]{:S(2)}) %all-to-all-start.6) | async-done | bytes 453280 | tf_op jit(solution)/shard_map/all_to_all | solution.py:36
  159.9 0.7 broadcast_in_dim.57
  160.6 3.4 %all-to-all-start.7 = ((f32[8,1,3541]{2,1,0:T(1,128)}), f32[8,1,3541]{2,1,0:T(1,128)S(1)}, u32[]{:S(2)}, u32[]{:S(2)}) async-start(f32[8,1,3541]{2,1,0:T(1,128)} %broadcast_in_dim.57), calls=%async_computation.7 | async-start | bytes 229376 | tf_op jit(solution)/shard_map/all_to_all | solution.py:36
  164.1 7.7 %all-to-all-done.7 = f32[8,1,3541]{2,1,0:T(1,128)S(1)} async-done(((f32[8,1,3541]{2,1,0:T(1,128)}), f32[8,1,3541]{2,1,0:T(1,128)S(1)}, u32[]{:S(2)}, u32[]{:S(2)}) %all-to-all-start.7) | async-done | bytes 113344 | tf_op jit(solution)/shard_map/all_to_all | solution.py:36
  172.0 0.6 slice.87
  172.7 0.8 multiply_reduce_fusion.2
  173.5 0.8 fusion.27
  177.3 0.8 multiply_reduce_fusion.5
  178.1 0.8 multiply_reduce_fusion.4
  178.8 1.1 fusion.28
  181.7 0.7 copy.87
  182.5 0.7 pad_maximum_fusion.8
  183.2 0.6 pad_maximum_fusion.12
  (81 shorter events, 8.1 us)
Async XLA Ops:
  0.6 4.2 %copy-start = (f32[58,8192]{1,0:T(8,128)S(1)}, f32[58,8192]{1,0:T(8,128)}, u32[]{:S(2)}) copy-start(f32[58,8192]{1,0:T(8,128)} %param.12) | copy-start | bytes 5701636
  2.1 10.5 %copy-start.3 = (s32[1,1,2,128]{3,2,1,0:T(2,128)S(1)}, s32[1,1,2,128]{3,2,1,0:T(2,128)}, u32[]{:S(2)}) copy-start(s32[1,1,2,128]{3,2,1,0:T(2,128)} %param.9) | copy-start | bytes 3076
  6.0 6.5 %collective-permute-start = (bf16[2,8192]{1,0:T(2,128)(2,1)S(1)}, bf16[2,8192]{1,0:T(2,128)(2,1)S(1)}, u32[]{:S(2)}, u32[]{:S(2)}) collective-permute-start(bf16[2,8192]{1,0:T(2,128)(2,1)S(1)} %pad_maximum_fusion.10), channel_id=1, source_target_pairs={{0,4},{4,8},{8,12},{12,16},{16,20},{20,24},{24,28},{28,32},{32,36}... | collective-permute-start | bytes 98312 | tf_op jit(solution)/shard_map/ppermute | solution.py:22
  10.6 5.2 %collective-permute-start.1 = (bf16[2,8192]{1,0:T(2,128)(2,1)S(1)}, bf16[2,8192]{1,0:T(2,128)(2,1)S(1)}, u32[]{:S(2)}, u32[]{:S(2)}) collective-permute-start(bf16[2,8192]{1,0:T(2,128)(2,1)S(1)} %pad_maximum_fusion.10), channel_id=1, source_target_pairs={{4,0},{8,4},{12,8},{16,12},{20,16},{24,20},{28,24},{32,28},{36,32}... | collective-permute-start | bytes 98312 | tf_op jit(solution)/shard_map/ppermute | solution.py:23
  17.0 11.0 %all-to-all-start = ((bf16[4,2,3,1,8192]{4,1,3,2,0:T(2,128)(2,1)}), bf16[4,2,3,1,8192]{4,1,3,2,0:T(2,128)(2,1)S(1)}, u32[]{:S(2)}, u32[]{:S(2)}) async-start(bf16[4,2,3,1,8192]{4,1,3,2,0:T(2,128)(2,1)} %broadcast_in_dim.51), calls=%async_computation | async-start | bytes 786432 | tf_op jit(solution)/shard_map/all_to_all | solution.py:36
  31.2 4.6 %copy-start.1 = (bf16[1,1,128,128,128]{4,3,2,1,0:T(8,128)(2,1)S(1)}, bf16[1,1,128,128,128]{4,3,2,1,0:T(8,128)(2,1)}, u32[]{:S(2)}) copy-start(bf16[1,1,128,128,128]{4,3,2,1,0:T(8,128)(2,1)} %param.7) | copy-start | bytes 12582916
  38.9 8.7 %all-to-all-start.1 = ((f32[4,1,8192]{2,1,0:T(1,128)}), f32[4,1,8192]{2,1,0:T(1,128)S(1)}, u32[]{:S(2)}, u32[]{:S(2)}) async-start(f32[4,1,8192]{2,1,0:T(1,128)} %bitcast.17), calls=%async_computation.1 | async-start | bytes 262144 | tf_op jit(solution)/shard_map/all_to_all | solution.py:51
  42.3 5.5 %copy-start.2 = (f32[8192]{0:T(1024)S(1)}, f32[8192]{0:T(1024)}, u32[]{:S(2)}) copy-start(f32[8192]{0:T(1024)} %param.10) | copy-start | bytes 98308
  69.8 15.8 %all-to-all-start.3 = ((f32[8,1,3423]{2,1,0:T(1,128)}), f32[8,1,3423]{2,1,0:T(1,128)S(1)}, u32[]{:S(2)}, u32[]{:S(2)}) async-start(f32[8,1,3423]{2,1,0:T(1,128)} %broadcast_in_dim.53), calls=%async_computation.3 | async-start | bytes 221184 | tf_op jit(solution)/shard_map/all_to_all | solution.py:36
  97.5 6.2 %collective-permute-start.2 = (bf16[2,8192]{1,0:T(2,128)(2,1)S(1)}, bf16[2,8192]{1,0:T(2,128)(2,1)S(1)}, u32[]{:S(2)}, u32[]{:S(2)}) collective-permute-start(bf16[2,8192]{1,0:T(2,128)(2,1)S(1)} %pad_maximum_fusion.11), channel_id=1, source_target_pairs={{0,4},{4,8},{8,12},{12,16},{16,20},{20,24},{24,28},{28,32},{32,36}... | collective-permute-start | bytes 98312 | tf_op jit(solution)/shard_map/ppermute | solution.py:22
  101.7 5.2 %collective-permute-start.3 = (bf16[2,8192]{1,0:T(2,128)(2,1)S(1)}, bf16[2,8192]{1,0:T(2,128)(2,1)S(1)}, u32[]{:S(2)}, u32[]{:S(2)}) collective-permute-start(bf16[2,8192]{1,0:T(2,128)(2,1)S(1)} %pad_maximum_fusion.11), channel_id=1, source_target_pairs={{4,0},{8,4},{12,8},{16,12},{20,16},{24,20},{28,24},{32,28},{36,32}... | collective-permute-start | bytes 98312 | tf_op jit(solution)/shard_map/ppermute | solution.py:23
  129.4 8.3 %all-to-all-start.5 = ((f32[4,1,8192]{2,1,0:T(1,128)}), f32[4,1,8192]{2,1,0:T(1,128)S(1)}, u32[]{:S(2)}, u32[]{:S(2)}) async-start(f32[4,1,8192]{2,1,0:T(1,128)} %bitcast.58), calls=%async_computation.5 | async-start | bytes 262144 | tf_op jit(solution)/shard_map/all_to_all | solution.py:51
  142.0 17.7 %all-to-all-start.6 = ((f32[32,1,3541]{2,1,0:T(1,128)}), f32[32,1,3541]{2,1,0:T(1,128)S(1)}, u32[]{:S(2)}, u32[]{:S(2)}) async-start(f32[32,1,3541]{2,1,0:T(1,128)} %broadcast_in_dim.56), calls=%async_computation.6 | async-start | bytes 917504 | tf_op jit(solution)/shard_map/all_to_all | solution.py:36
  160.6 11.2 %all-to-all-start.7 = ((f32[8,1,3541]{2,1,0:T(1,128)}), f32[8,1,3541]{2,1,0:T(1,128)S(1)}, u32[]{:S(2)}, u32[]{:S(2)}) async-start(f32[8,1,3541]{2,1,0:T(1,128)} %broadcast_in_dim.57), calls=%async_computation.7 | async-start | bytes 229376 | tf_op jit(solution)/shard_map/all_to_all | solution.py:36
where the time goes:
time: 185 us; the launch traced here: 184 us
  waiting for transfers between devices  44.8 us (24%)
  starting transfers between devices  42 us (23%)
  matrix products  41.1 us (22%)
  blocking collectives  26.8 us (14%)
  local copies, waits for them, and re-layouts  16.1 us (9%)
  between operations  8.39 us (5%)
  other arithmetic  4.57 us (2%)
    all_to_all x4, waiting for transfers between devices, from_everyone(): return lax.all_to_all(copies, axis, split_axis=0, concat_axis=0, tiled=True)  32.6 us
    all_to_all x2, blocking collectives, from_everyone(): return lax.all_to_all(copies, axis, split_axis=0, concat_axis=0, tiled=True)  26.8 us
    all_to_all x4, starting transfers between devices, from_everyone(): return lax.all_to_all(copies, axis, split_axis=0, concat_axis=0, tiled=True)  22.4 us
    dot_general x2, matrix products, tile_products(): jnp.einsum('sij,sj->si', damping, picked_damp, preferred_element_type=jnp...  9.01 us
    ppermute x2, starting transfers between devices, padded(): before = lax.ppermute(last, axis, up)  8.85 us
    all_to_all x2, starting transfers between devices, sent_and_summed(): lax.all_to_all(blocks, axis, split_axis=0, concat_axis=0, tiled=True)  6.87 us
    dot_general x2, matrix products, tile_products(): jnp.einsum('sij,sj->si', stiffness, picked_stiff, preferred_element_type=...  6.71 us
    ppermute x2, waiting for transfers between devices, padded(): after = lax.ppermute(initial, axis, down)  6.57 us
  transfers between devices with their start and end apart: 10, of which 8 were waited for; matrix products, arithmetic and copies ran while one was open for 2% of the time, Pallas kernels for 0%

commit v1 on v0

v1 whole, which is shorter than its diff:
```python
import functools

import jax
import jax.numpy as jnp
from jax import lax
from jax.experimental import pallas as pl
from jax.experimental.pallas import tpu as pltpu
from jax.sharding import PartitionSpec as P

ITERS = 2
EPS = 1e-06
GROUP = 16
MESH = pl.DeviceIdType.MESH
F32 = jnp.float32
BF16 = jnp.bfloat16


def dot_nt(a, b):
    return lax.dot_general(a, b, (((1,), (1,)), ((), ())), preferred_element_type=F32)


def halves(x):
    hi = x.astype(BF16)
    return hi, (x - hi.astype(F32)).astype(BF16)


def iota(shape, dim):
    return lax.broadcasted_iota(jnp.int32, shape, dim)


def lane_sum(x):
    return jnp.sum(x, axis=1, keepdims=True)


def row_sum(x):
    return jnp.sum(x, axis=0, keepdims=True)


class Plan:
    def __init__(self, rows, subs):
        self.rows, self.subs = rows, subs
        self.cores = 2
        self.ys = 4 if rows >= 32 else 2
        self.zs = rows // (self.ys * self.cores)
        self.plane = self.ys * subs
        self.line = self.zs * self.cores


def body(
    plan, k0, j0, unknowns, slots, tile_rows,
    stiff_hbm, damp_hbm, map_ref, mass_ref, shift_ref, basis_hbm, compact_ref,
    new_ref, comp_ref, hess_ref,
    tiles_d, tiles_k, nat, held, image_s, column_s, coef_u, coef_l, upper_m, lower_m, gram_m,
    split_s, onehot_g, onehot_s, window, part_s, part_r, parts_m, plane_r, line_r,
    gram_s, gram_1, gram_2, gram_3,
    tile_sem, basis_sem, send_sem, recv_sem,
):
    rows, subs = plan.rows, plan.subs
    row = lax.axis_index("rows")
    sub = lax.axis_index("sub")
    core = lax.rem(row, plan.cores)
    chip = lax.div(row, plan.cores)
    y = lax.rem(chip, plan.ys)
    z = lax.div(chip, plan.ys)
    in_plane = y * subs + sub
    in_line = z * plan.cores + core
    above = lax.rem(row + rows - 1, rows)
    below = lax.rem(row + 1, rows)

    def plane_peer(step):
        peer = lax.rem(in_plane + step, plan.plane)
        to_y, to_x = lax.div(peer, subs), lax.rem(peer, subs)
        return peer, ((z * plan.ys + to_y) * plan.cores + core, to_x)

    def line_peer(step):
        peer = lax.rem(in_line + step, plan.line)
        to_z, to_core = lax.div(peer, plan.cores), lax.rem(peer, plan.cores)
        return peer, ((to_z * plan.ys + y) * plan.cores + to_core, sub)

    barrier = pltpu.get_barrier_semaphore()

    def greet(device):
        pl.semaphore_signal(barrier, inc=1, device_id=device, device_id_type=MESH)

    def greet_plane(step, carry):
        greet(plane_peer(step)[1])
        return carry

    def greet_line(step, carry):
        greet(line_peer(step)[1])
        return carry

    def greet_beside(step, carry):
        greet((above, step))
        greet((below, step))
        return carry

    basis_copy = pltpu.make_async_copy(basis_hbm, nat, basis_sem)
    basis_copy.start()
    lax.fori_loop(0, subs, greet_beside, 0)
    lax.fori_loop(1, plan.plane, greet_plane, 0)
    lax.fori_loop(1, plan.line, greet_line, 0)
    copies = []
    for i, (hbm, ref) in enumerate(((damp_hbm, tiles_d), (stiff_hbm, tiles_k))):
        copy = pltpu.make_async_copy(hbm, ref, tile_sem.at[i])
        copy.start()
        copies.append(copy)

    def send(src, dst, which, device):
        pltpu.make_async_remote_copy(
            src_ref=src, dst_ref=dst, send_sem=send_sem.at[which], recv_sem=recv_sem.at[which],
            device_id=device, device_id_type=MESH,
        ).start()

    def arrived(view, which):
        pltpu.make_async_copy(view, view, recv_sem.at[which]).wait()

    def departed(view, which):
        pltpu.make_async_copy(view, view, send_sem.at[which]).wait()

    shift = shift_ref[0]
    scale = 1.0 / unknowns
    eye = (iota((128, 128), 0) == iota((128, 128), 1)).astype(F32)
    eye64 = (iota((64, 128), 0) == iota((64, 128), 1)).astype(F32)
    lane = iota((1, 128), 1)
    lane64 = iota((64, 128), 1)
    row64 = iota((64, 128), 0)

    upper_m[...] = jnp.zeros_like(upper_m)
    lower_m[...] = jnp.zeros_like(lower_m)
    upper_m[0:k0, 0:j0] = compact_ref[0]
    lower_m[0:k0, 0:j0] = compact_ref[1]
    u1 = lane_sum(jnp.where(lane64 == j0 - 1, upper_m[...], 0.0))
    u2 = lane_sum(jnp.where(lane64 == j0 - 1, lower_m[...], 0.0))
    u1 = jnp.broadcast_to(u1, (64, 128))
    u2 = jnp.broadcast_to(u2, (64, 128))
    coef_u[...] = u1
    coef_l[...] = u2
    column_s[...] = jnp.zeros_like(column_s)
    parts_m[...] = jnp.zeros_like(parts_m)
    split_s[...] = jnp.zeros_like(split_s)

    basis_copy.wait()
    nt = tile_rows

    def regroup(t, carry):
        held[pl.ds(t, k0, stride=nt), :] = nat[:, pl.ds(pl.multiple_of(t * 128, 128), 128)]
        return carry

    lax.fori_loop(0, nt, regroup, 0)

    def held_row(k):
        return held[pl.ds(pl.multiple_of(k * nt, 8), nt), :]

    def combined(refs):
        def add(k, totals):
            h = held_row(k)
            return tuple(
                total + h * jnp.broadcast_to(ref[pl.ds(k, 1), :], h.shape)
                for total, ref in zip(totals, refs)
            )
        return lax.fori_loop(0, k0, add, tuple(jnp.zeros((nt, 128), F32) for _ in refs))

    def exchange(it, upper, lower):
        mine = window.at[it, subs + sub]
        mine[...] = jnp.concatenate([upper, lower], axis=1).astype(BF16)
        which = it
        for step in range(1, subs):
            to = lax.rem(sub + step, subs)
            send(mine, window.at[it, subs + sub], which, (row, to))
        for step in range(subs):
            to = lax.rem(sub + step, subs)
            send(mine, window.at[it, sub], which, (below, to))
            send(mine, window.at[it, 2 * subs + sub], which, (above, to))

    upper, lower = combined((coef_u, coef_l))
    pl.semaphore_wait(barrier, plan.plane + plan.line - 2 + 2 * subs)
    exchange(0, upper, lower)

    wide = nat.shape[1] // 8

    def gram_part(c, total):
        piece = nat[:, pl.ds(pl.multiple_of(c * wide, 128), wide)]
        hi, lo = halves(piece)
        split_s[0:k0, :] = hi
        split_s[64 : 64 + k0, :] = lo
        return total + dot_nt(split_s[...], split_s[0:64, :])

    both = lax.fori_loop(0, 8, gram_part, jnp.zeros((128, 64), F32))
    cross = both[64:128]
    gram = both[0:64] + cross + cross.T
    gram = jnp.concatenate([gram, jnp.zeros((64, 64), F32)], axis=1)
    chunk = 64 // plan.plane
    for p in range(plan.plane):
        gram_s[p] = gram[p * chunk : (p + 1) * chunk]
    gram_1[in_plane] = gram_s[in_plane]

    def gram_out(step, carry):
        peer, device = plane_peer(step)
        send(gram_s.at[peer], gram_1.at[in_plane], 8, device)
        return carry

    lax.fori_loop(1, plan.plane, gram_out, 0)

    target = map_ref[0:1, :].astype(F32)
    source = map_ref[1:2, :].astype(F32)
    onehot_s[...] = (
        jnp.broadcast_to(target, onehot_s.shape) == iota(onehot_s.shape, 0).astype(F32)
    ).astype(F32).astype(BF16)
    eye_s = (iota((slots, slots), 0) == iota((slots, slots), 1)).astype(F32)
    source_col = lane_sum(jnp.broadcast_to(source, (slots, slots)) * eye_s)
    spot = iota(onehot_g.shape, 1)
    first_tile = jnp.where(row == 0, subs * nt, 0)
    last_tile = jnp.where(row == rows - 1, 2 * subs * nt, 3 * subs * nt)
    hit = (
        (jnp.broadcast_to(source_col, onehot_g.shape) == spot.astype(F32))
        & (spot >= first_tile) & (spot < last_tile)
    )
    onehot_g[...] = hit.astype(F32).astype(BF16)
    mass = mass_ref[...]
    block = min(16, slots)
    lane_s = iota((128, slots), 1)

    for it in range(ITERS):
        m, cols = k0 + it, j0 + it
        others = window.at[it, pl.ds(0, 3 * subs - 1)]
        arrived(others, it)
        departed(others, it)
        picked = jnp.dot(
            onehot_g[...], window[it].reshape(3 * subs * nt, 256), preferred_element_type=F32
        ).astype(BF16)
        if it == 0:
            for copy in copies:
                copy.wait()

        def products(b, total):
            d = tiles_d[pl.ds(b * block, block)].reshape(block * 128, 128)
            k = tiles_k[pl.ds(b * block, block)].reshape(block * 128, 128)
            r = dot_nt(jnp.concatenate([d, k], axis=1), picked)
            for i in range(block):
                total = jnp.where(lane_s == b * block + i, r[i * 128 : (i + 1) * 128], total)
            return total

        product = lax.fori_loop(0, slots // block, products, jnp.zeros((128, slots), F32))
        hi, lo = halves(product)
        part = dot_nt(onehot_s[...], hi) + dot_nt(onehot_s[...], lo)
        part_s[it] = part.reshape(subs, nt, 128)
        for step in range(1, subs):
            to = lax.rem(sub + step, subs)
            send(part_s.at[it, to], part_r.at[it, step - 1], 2 + it, (row, to))
        if it == 0:
            rest = gram_1.at[pl.ds(0, plan.plane - 1)]
            arrived(rest, 8)
            departed(rest, 8)
            gram_2[in_line] = jnp.sum(gram_1[...], axis=0)

            def gram_on(step, carry):
                send(gram_2.at[in_line], gram_2.at[in_line], 9, line_peer(step)[1])
                return carry

            lax.fori_loop(1, plan.line, gram_on, 0)
        own = part_s[it, sub]
        arrived(part_r.at[it], 2 + it)
        departed(part_r.at[it], 2 + it)
        coupled = own + part_r[it, 0]
        for step in range(2, subs):
            coupled = coupled + part_r[it, step - 1]
        image = shift * upper - mass * coupled
        image_s[...] = image
        if it == 0:
            rest = gram_2.at[pl.ds(0, plan.line - 1)]
            arrived(rest, 9)
            departed(rest, 9)
            gram_3[in_plane] = jnp.sum(gram_2[...], axis=0)

            def gram_back(step, carry):
                send(gram_3.at[in_plane], gram_3.at[in_plane], 10, plane_peer(step)[1])
                return carry

            lax.fori_loop(1, plan.plane, gram_back, 0)

        def inner(t, total):
            piece = nat[:, pl.ds(pl.multiple_of(t * 128, 128), 128)]
            return total + piece * jnp.broadcast_to(image_s[pl.ds(t, 1), :], piece.shape)

        parts_m[0:k0, :] = lax.fori_loop(0, nt, inner, jnp.zeros((k0, 128), F32))
        if it > 0:
            parts_m[k0 : k0 + 1, :] = row_sum(column_s[...] * image)
        parts_m[63:64, :] = row_sum(image * image)
        line = row_sum(parts_m[...].T)
        plane_r[it, in_plane] = line

        def plane_out(step, carry):
            spot = plane_r.at[it, in_plane]
            send(spot, spot, 4 + it, plane_peer(step)[1])
            return carry

        lax.fori_loop(1, plan.plane, plane_out, 0)
        if it == 0:
            rest = gram_3.at[pl.ds(0, plan.plane - 1)]
            arrived(rest, 10)
            departed(rest, 10)
            gram_m[...] = gram_3[...].reshape(64, 128) * scale
        rest = plane_r.at[it, pl.ds(0, plan.plane - 1)]
        arrived(rest, 4 + it)
        departed(rest, 4 + it)
        line_r[it, in_line] = jnp.sum(plane_r[it], axis=0)

        def line_out(step, carry):
            spot = line_r.at[it, in_line]
            send(spot, spot, 6 + it, line_peer(step)[1])
            return carry

        lax.fori_loop(1, plan.line, line_out, 0)
        gram = gram_m[...]
        rest = line_r.at[it, pl.ds(0, plan.line - 1)]
        arrived(rest, 6 + it)
        departed(rest, 6 + it)
        sums = jnp.sum(line_r[it], axis=0) * scale

        own_square = lane_sum(jnp.where(lane == 63, sums, 0.0))
        first = jnp.where(lane < m, sums, 0.0)
        coef = lane_sum((2.0 * eye64 - gram) * first)
        coef = jnp.broadcast_to(coef, (64, 128))
        coef_row = row_sum(eye64 * coef)
        gram_coef = row_sum(gram * coef)
        square = own_square + lane_sum(coef_row * (gram_coef - 2.0 * first))
        norm = jnp.sqrt(square + EPS)

        up, low = upper_m[...], lower_m[...]
        upper_c = jnp.where(row64 == m, norm, coef)
        lower_c = u1 + shift * u2
        weights = jnp.zeros((1, 128), F32)
        for _ in range(2):
            projection = row_sum(up * upper_c + low * lower_c)
            upper_c = upper_c - lane_sum(up * projection)
            lower_c = lower_c - lane_sum(low * projection)
            weights = weights + projection
        beta = jnp.sqrt(
            row_sum(upper_c * upper_c) + row_sum(lower_c * lower_c) + EPS
        )
        u1, u2 = upper_c / beta, lower_c / beta
        weights = jnp.where(lane == cols, beta, weights)
        hess = lane_sum(eye64 * weights)
        hess_ref[:, it : it + 1] = hess[0 : j0 + ITERS]

        if it + 1 < ITERS:
            tail = row_sum(jnp.where(row64 == m, u1, 0.0))
            ratio = tail / norm
            coef_u[...] = u1 - ratio * coef
            coef_l[...] = u2
            held_u, lower = combined((coef_u, coef_l))
            upper = held_u + ratio * image
            exchange(it + 1, upper, lower)
        up = jnp.where(lane64 == cols, u1, up)
        low = jnp.where(lane64 == cols, u2, low)
        upper_m[...] = up
        lower_m[...] = low
        coef_u[...] = coef
        (taken,) = combined((coef_u,))
        if it > 0:
            taken = taken + row_sum(jnp.where(row64 == k0, coef, 0.0)) * column_s[...]
        column_s[...] = (image - taken) / norm
        for t in range(nt):
            new_ref[it : it + 1, t * 128 : (t + 1) * 128] = column_s[t : t + 1, :]
        if it + 1 < ITERS:
            cross_row = (first - gram_coef) / norm
            cross_col = lane_sum(eye64 * cross_row)
            gram = jnp.where(row64 == m, cross_row, gram)
            gram = jnp.where(lane64 == m, cross_col, gram)
            gram = jnp.where((row64 == m) & (lane64 == m), square / (norm * norm), gram)
            gram_m[...] = gram
    comp_ref[0] = upper_m[0 : k0 + ITERS, 0 : j0 + ITERS]
    comp_ref[1] = lower_m[0 : k0 + ITERS, 0 : j0 + ITERS]


def on_device(stiffness, damping, tile_map, mass, shift, basis, compact, *, rows, subs):
    plan = Plan(rows, subs)
    k0, local = basis.shape
    j0 = compact.shape[2]
    slots = stiffness.shape[2]
    nt = local // 128
    unknowns = local * rows * subs
    chunk = 64 // plan.plane
    vmem = pl.BlockSpec(memory_space=pltpu.VMEM)
    hbm = pl.BlockSpec(memory_space=pl.ANY)
    smem = pl.BlockSpec(memory_space=pltpu.SMEM)
    scratch = [
        pltpu.VMEM((slots, 128, 128), BF16),
        pltpu.VMEM((slots, 128, 128), BF16),
        pltpu.VMEM((k0, local), F32),
        pltpu.VMEM((k0 * nt, 128), F32),
        pltpu.VMEM((nt, 128), F32),
        pltpu.VMEM((nt, 128), F32),
        pltpu.VMEM((64, 128), F32),
        pltpu.VMEM((64, 128), F32),
        pltpu.VMEM((64, 128), F32),
        pltpu.VMEM((64, 128), F32),
        pltpu.VMEM((64, 128), F32),
        pltpu.VMEM((128, local // 8), BF16),
        pltpu.VMEM((slots, 3 * subs * nt), BF16),
        pltpu.VMEM((subs * nt, slots), BF16),
        pltpu.VMEM((ITERS, 3 * subs, nt, 256), BF16),
        pltpu.VMEM((ITERS, subs, nt, 128), F32),
        pltpu.VMEM((ITERS, subs - 1, nt, 128), F32),
        pltpu.VMEM((128, 128), F32),
        pltpu.VMEM((ITERS, plan.plane, 1, 128), F32),
        pltpu.VMEM((ITERS, plan.line, 1, 128), F32),
        pltpu.VMEM((plan.plane, chunk, 128), F32),
        pltpu.VMEM((plan.plane, chunk, 128), F32),
        pltpu.VMEM((plan.line, chunk, 128), F32),
        pltpu.VMEM((plan.plane, chunk, 128), F32),
        pltpu.SemaphoreType.DMA((2,)),
        pltpu.SemaphoreType.DMA,
        pltpu.SemaphoreType.DMA((11,)),
        pltpu.SemaphoreType.DMA((11,)),
    ]
    outs = pl.pallas_call(
        functools.partial(body, plan, k0, j0, unknowns, slots, nt),
        out_shape=(
            jax.ShapeDtypeStruct((ITERS, local), F32),
            jax.ShapeDtypeStruct((2, k0 + ITERS, j0 + ITERS), F32),
            jax.ShapeDtypeStruct((j0 + ITERS, ITERS), F32),
        ),
        in_specs=[hbm, hbm, vmem, vmem, smem, hbm, vmem],
        out_specs=(vmem, vmem, vmem),
        scratch_shapes=scratch,
        compiler_params=pltpu.CompilerParams(
            collective_id=0, has_side_effects=True, vmem_limit_bytes=48 << 20
        ),
        name="toar",
    )(
        stiffness.reshape(stiffness.shape[2:]), damping.reshape(damping.shape[2:]),
        tile_map.reshape(2, slots), mass.reshape(nt, 128), shift.reshape(1), basis, compact,
    )
    return outs


def solution(mesh):
    rows, subs = mesh.shape["rows"], mesh.shape["sub"]
    both = ("rows", "sub")
    return jax.shard_map(
        functools.partial(on_device, rows=rows, subs=subs),
        mesh=mesh,
        in_specs=(
            P("rows", "sub", None, None, None), P("rows", "sub", None, None, None),
            P("rows", "sub", None, None), P(both), P(), P(None, both), P(),
        ),
        out_specs=(P(None, both), P(), P()),
        check_vma=False,
    )
```

time: 185 us -> 70.4 us (0.38)
  Pallas kernels: 0 us -> 62.9 us
  waiting for transfers between devices: 44.8 us -> 0 us
  starting transfers between devices: 42 us -> 0 us
  matrix products: 41.1 us -> 0 us
  blocking collectives: 26.8 us -> 0 us
  local copies, waits for them, and re-layouts: 16.1 us -> 5.94 us
  between operations: 8.39 us -> 1.29 us
  other arithmetic: 4.57 us -> 0 us
    pallas_call x0 -> x1, Pallas kernels: none -> 62.9 us  [on_device(): pl.pallas_call(functools.partial(body, plan, k0, j0, unknowns, slots, nt)...]
    dot_general x36 -> x0, matrix products: 41.1 us -> none  [the longest x2 9.01 us: tile_products(): jnp.einsum('sij,sj->si', damping, picked_damp, preferred_element_type=jnp...]
    all_to_all x6 -> x0, waiting for transfers between devices: 38.2 us -> none  [the longest x4 32.6 us: from_everyone(): return lax.all_to_all(copies, axis, split_axis=0, concat_axis=0, tiled=True)]
    all_to_all x6 -> x0, starting transfers between devices: 29.3 us -> none  [the longest x4 22.4 us: from_everyone(): return lax.all_to_all(copies, axis, split_axis=0, concat_axis=0, tiled=True)]
    all_to_all x2 -> x0, blocking collectives: 26.8 us -> none  [from_everyone(): return lax.all_to_all(copies, axis, split_axis=0, concat_axis=0, tiled=True)]
    ppermute x4 -> x0, starting transfers between devices: 12.7 us -> none  [the longest x2 8.85 us: padded(): before = lax.ppermute(last, axis, up)]
    ppermute x4 -> x0, waiting for transfers between devices: 6.57 us -> none  [the longest x2 6.57 us: padded(): after = lax.ppermute(initial, axis, down)]
    slice x10 -> x0, local copies, waits for them, and re-layouts: 5.02 us -> none  [the longest x4 2.07 us: tile_products(): picked_stiff = blocked[1][source]]
  transfers between devices with their start and end apart: 10 -> 0, of which waited for: 8 -> 0; matrix products, arithmetic and copies ran while one was open for 2% -> 0% of each run, Pallas kernels for 0% -> 0%
where the time goes in v1:
time: 70.4 us; the launch traced here: 70.1 us
  Pallas kernels  62.9 us (89%)
  local copies, waits for them, and re-layouts  5.94 us (8%)
  between operations  1.29 us (2%)
    pallas_call x1, Pallas kernels, on_device(): pl.pallas_call(functools.partial(body, plan, k0, j0, unknowns, slots, nt)...  62.9 us
    unnamed x8, local copies, waits for them, and re-layouts  4.58 us

profile of v1, /device:TPU:1, one launch (start us, length us, event | category | flops | bytes accessed | tf_op | source)
XLA Modules:
  0.0 70.1 jit_solution(3685625890331492050)
XLA Ops:
  1.3 0.9 %copy.10.compact_ref = f32[2,58,57]{2,1,0:T(8,128)S(1)} copy(f32[2,58,57]{1,0,2:T(2,128)} %param.13) | data formatting | bytes 52896 | tf_op args[6]
  2.2 0.0 copy-start
  2.2 1.6 %copy-done = f32[58,8192]{1,0:T(8,128)S(1)} copy-done((f32[58,8192]{1,0:T(8,128)S(1)}, f32[58,8192]{1,0:T(8,128)}, u32[]{:S(2)}) %copy-start) | copy-done | bytes 1900568
  3.8 0.0 copy-start.1
  3.8 0.8 %copy-done.1 = f32[8192]{0:T(1024)S(1)} copy-done((f32[8192]{0:T(1024)S(1)}, f32[8192]{0:T(1024)}, u32[]{:S(2)}) %copy-start.1) | copy-done | bytes 32792
  4.6 0.0 copy-start.2
  4.6 0.7 copy-done.2
  5.2 62.9 %toar.1 = (f32[2,8192]{1,0:T(2,128)S(1)}, f32[2,60,59]{2,1,0:T(8,128)S(1)}, f32[59,2]{1,0:T(8,128)S(1)}) custom-call(bf16[128,128,128]{2,1,0:T(8,128)(2,1)} %bitcast.8, bf16[128,128,128]{2,1,0:T(8,128)(2,1)} %bitcast.9, s32[2,128]{1,0:T(2,128)S(1)} %bitcast.7, f32[64,128]{1,0:T(8,128)S(1)} %bitcast.6, f32[1]{0:T(128)} %bitcast.5.shift_ref, ...), custom_call_target="tpu_custom_call" | custom-call | tf_op jit(solution)/shard_map/toar/pallas_call | solution.py:418
  68.1 0.6 copy.12
  68.8 0.7 %copy.11 = f32[2,60,59]{1,0,2:T(2,128)} copy(f32[2,60,59]{2,1,0:T(8,128)S(1)} %get-tuple-element.4) | data formatting | bytes 56640 | tf_op jit(solution)/shard_map/toar/pallas_call | solution.py:418
  69.5 0.6 copy.15
Async XLA Ops:
  2.2 1.6 %copy-start = (f32[58,8192]{1,0:T(8,128)S(1)}, f32[58,8192]{1,0:T(8,128)}, u32[]{:S(2)}) copy-start(f32[58,8192]{1,0:T(8,128)} %basis_hbm.1) | copy-start | bytes 5701636
  3.8 0.8 %copy-start.1 = (f32[8192]{0:T(1024)S(1)}, f32[8192]{0:T(1024)}, u32[]{:S(2)}) copy-start(f32[8192]{0:T(1024)} %param.10) | copy-start | bytes 98308
  4.6 0.7 copy-start.2

commit v2 on v1

v2 whole, which is shorter than its diff:
```python
import functools
import itertools

import jax
import jax.numpy as jnp
from jax import lax
from jax.experimental import pallas as pl
from jax.experimental.pallas import tpu as pltpu
from jax.sharding import PartitionSpec as P

ITERS = 2
EPS = 1e-06
MESH = pl.DeviceIdType.MESH
F32 = jnp.float32
BF16 = jnp.bfloat16
HELD = 60


def dot_nt(a, b):
    return lax.dot_general(a, b, (((1,), (1,)), ((), ())), preferred_element_type=F32)


def halves(x):
    hi = x.astype(BF16)
    return hi, (x - hi.astype(F32)).astype(BF16)


def iota(shape, dim):
    return lax.broadcasted_iota(jnp.int32, shape, dim)


def lane_sum(x):
    return jnp.sum(x, axis=1, keepdims=True)


def row_sum(x):
    return jnp.sum(x, axis=0, keepdims=True)


def tree_sum(terms):
    while len(terms) > 1:
        terms = [sum(terms[i + 1 : i + 2], terms[i]) for i in range(0, len(terms), 2)]
    return terms[0]


def ring_distance(step, size):
    return min(step, size - step)


class Plan:
    def __init__(self, rows, subs):
        self.rows, self.subs = rows, subs
        self.cores = 2
        self.ys = 4 if rows >= 32 else 2
        self.zs = rows // (self.ys * self.cores)
        self.plane = self.ys * subs
        self.line = self.zs * self.cores
        self.cube = self.zs * self.ys * subs

    def steps(self, *sizes):
        every = [s for s in itertools.product(*map(range, sizes)) if any(s)]
        return sorted(every, key=lambda s: -sum(map(ring_distance, s, sizes)))


def body(
    plan, k0, j0, unknowns, slots, nt,
    stiff_hbm, damp_hbm, map_hbm, mass_hbm, shift_ref, basis_hbm, compact_hbm,
    new_ref, comp_ref, hess_ref,
    tiles_d, tiles_k, nat, held, map_s, mass_s, compact_s, image_s, column_s, coef_u, coef_l,
    square_s, upper_m, lower_m, gram_m, split_s, onehot_g, onehot_s, window, part_s, part_r,
    parts_m, pair_r, cube_r, gram_s, gram_1, gram_2, gram_3,
    copy_sem, send_sem, recv_sem, ready_sem,
):
    rows, subs = plan.rows, plan.subs
    basis_copy = pltpu.make_async_copy(basis_hbm, nat, copy_sem.at[0])
    basis_copy.start()

    row = lax.axis_index("rows")
    sub = lax.axis_index("sub")
    core = lax.rem(row, plan.cores)
    chip = lax.div(row, plan.cores)
    y = lax.rem(chip, plan.ys)
    z = lax.div(chip, plan.ys)
    in_plane = y * subs + sub
    in_line = z * plan.cores + core
    in_cube = chip * subs + sub
    to_x = [lax.rem(sub + i, subs) for i in range(subs)]
    to_y = [lax.rem(y + i, plan.ys) for i in range(plan.ys)]
    to_z = [lax.rem(z + i, plan.zs) for i in range(plan.zs)]
    to_c = [core, 1 - core]
    above = lax.rem(row + rows - 1, rows)
    below = lax.rem(row + 1, rows)

    def at(dz, dy, dc, dx):
        return ((to_z[dz] * plan.ys + to_y[dy]) * plan.cores + to_c[dc], to_x[dx])

    plane_peers = [
        (to_y[dy] * subs + to_x[dx], at(0, dy, 0, dx)) for dy, dx in plan.steps(plan.ys, subs)
    ]
    line_peers = [at(dz, 0, dc, 0) for dz, dc in plan.steps(plan.zs, plan.cores)]
    beside = [
        (device, to_x[dx])
        for dx in sorted(range(subs), key=lambda i: -ring_distance(i, subs))
        for device in (above, below)
    ]

    barrier = pltpu.get_barrier_semaphore()
    greeted = line_peers + beside + [device for _, device in plane_peers]
    for device in greeted:
        pl.semaphore_signal(barrier, inc=1, device_id=device, device_id_type=MESH)

    small = [
        pltpu.make_async_copy(compact_hbm, compact_s, copy_sem.at[1]),
        pltpu.make_async_copy(map_hbm, map_s, copy_sem.at[2]),
        pltpu.make_async_copy(mass_hbm, mass_s, copy_sem.at[3]),
    ]
    for copy in small:
        copy.start()

    def send(src, dst, which, device):
        pltpu.make_async_remote_copy(
            src_ref=src, dst_ref=dst, send_sem=send_sem.at[which], recv_sem=recv_sem.at[which],
            device_id=device, device_id_type=MESH,
        ).start()

    def arrived(view, which):
        pltpu.make_async_copy(view, view, recv_sem.at[which]).wait()

    def departed(view, which):
        pltpu.make_async_copy(view, view, send_sem.at[which]).wait()

    shift = shift_ref[0]
    scale = 1.0 / unknowns
    eye64 = (iota((64, 128), 0) == iota((64, 128), 1)).astype(F32)
    lane = iota((1, 128), 1)
    lane64 = iota((64, 128), 1)
    row64 = iota((64, 128), 0)
    column_s[...] = jnp.zeros_like(column_s)
    parts_m[...] = jnp.zeros_like(parts_m)
    split_s[...] = jnp.zeros_like(split_s)
    held[k0 * nt :, :] = jnp.zeros((held.shape[0] - k0 * nt, 128), F32)

    small[0].wait()
    for matrix, which in ((upper_m, 0), (lower_m, 1)):
        square_s[...] = jnp.zeros_like(square_s)
        square_s[0:j0, 0:k0] = compact_s[:, which, :]
        matrix[...] = square_s[...].T[0:64]
    comp_ref[...] = jnp.zeros_like(comp_ref)
    comp_ref[0:j0, :, 0:k0] = compact_s[...]
    u1 = jnp.broadcast_to(lane_sum(jnp.where(lane64 == j0 - 1, upper_m[...], 0.0)), (64, 128))
    u2 = jnp.broadcast_to(lane_sum(jnp.where(lane64 == j0 - 1, lower_m[...], 0.0)), (64, 128))
    coef_u[...] = u1
    coef_l[...] = u2

    basis_copy.wait()
    tile_copies = [
        pltpu.make_async_copy(damp_hbm, tiles_d, copy_sem.at[4]),
        pltpu.make_async_copy(stiff_hbm, tiles_k, copy_sem.at[5]),
    ]
    for copy in tile_copies:
        copy.start()

    def regroup(b, carry):
        for i in range(4):
            t = b * 4 + i
            held[pl.ds(t, k0, stride=nt), :] = nat[:, pl.ds(pl.multiple_of(t * 128, 128), 128)]
        return carry

    lax.fori_loop(0, nt // 4, regroup, 0)

    def combined(refs):
        def add(b, totals):
            for i in range(4):
                k = b * 4 + i
                h = held[pl.ds(pl.multiple_of(k * nt, 8), nt), :]
                totals = tuple(
                    total + h * jnp.broadcast_to(ref[pl.ds(k, 1), :], h.shape)
                    for total, ref in zip(totals, refs)
                )
            return totals
        return lax.fori_loop(0, HELD // 4, add, tuple(jnp.zeros((nt, 128), F32) for _ in refs))

    def pack(it, upper, lower):
        window[it, subs + sub] = jnp.concatenate([upper, lower], axis=1).astype(BF16)

    def exchange(it):
        mine = window.at[it, subs + sub]
        for device in beside:
            place = sub if device[0] is below else 2 * subs + sub
            send(mine, window.at[it, place], it, device)
        for step in range(1, subs):
            send(mine, mine, it, (row, to_x[step]))

    upper, lower = combined((coef_u, coef_l))
    pack(0, upper, lower)

    wide = nat.shape[1] // 8

    def gram_part(c, total):
        piece = nat[:, pl.ds(pl.multiple_of(c * wide, 128), wide)]
        hi, lo = halves(piece)
        split_s[0:k0, :] = hi
        split_s[64 : 64 + k0, :] = lo
        return total + dot_nt(split_s[...], split_s[0:64, :])

    def gram_ready():
        both = lax.fori_loop(0, 8, gram_part, jnp.zeros((128, 64), F32))
        cross = both[64:128]
        gram = both[0:64] + cross + cross.T
        gram = jnp.concatenate([gram, jnp.zeros((64, 64), F32)], axis=1)
        chunk = 64 // plan.plane
        for p in range(plan.plane):
            gram_s[p] = gram[p * chunk : (p + 1) * chunk]
        gram_1[in_plane] = gram_s[in_plane]

    small[1].wait()
    small[2].wait()
    target = map_s[0:1, :].astype(F32)
    source = map_s[1:2, :].astype(F32)
    onehot_s[...] = (
        jnp.broadcast_to(target, onehot_s.shape) == iota(onehot_s.shape, 0).astype(F32)
    ).astype(F32).astype(BF16)
    eye_s = (iota((slots, slots), 0) == iota((slots, slots), 1)).astype(F32)
    source_col = lane_sum(jnp.broadcast_to(source, (slots, slots)) * eye_s)
    spot = iota(onehot_g.shape, 1)
    first_tile = jnp.where(row == 0, subs * nt, 0)
    last_tile = jnp.where(row == rows - 1, 2 * subs * nt, 3 * subs * nt)
    hit = (
        (jnp.broadcast_to(source_col, onehot_g.shape) == spot.astype(F32))
        & (spot >= first_tile) & (spot < last_tile)
    )
    onehot_g[...] = hit.astype(F32).astype(BF16)
    gram_ready()

    pl.semaphore_wait(barrier, len(greeted))
    exchange(0)
    for _, device in plane_peers:
        pl.semaphore_signal(ready_sem, inc=1, device_id=device, device_id_type=MESH)
    for peer, device in plane_peers:
        send(gram_s.at[peer], gram_1.at[in_plane], 8, device)

    mass = mass_s[...]
    block = min(64, slots)
    lane_s = iota((128, slots), 1)
    plane_view = pl.ds(0, plan.plane - 1)
    line_view = pl.ds(0, plan.line - 1)
    cube_view = pl.ds(0, plan.cube - 1)

    for it in range(ITERS):
        m, cols = k0 + it, j0 + it
        arrived(window.at[it, pl.ds(0, 3 * subs - 1)], it)
        picked = jnp.dot(
            onehot_g[...], window[it].reshape(3 * subs * nt, 256), preferred_element_type=F32
        ).astype(BF16)
        if it == 0:
            for copy in tile_copies:
                copy.wait()

        def products(b, total):
            d = tiles_d[pl.ds(b * block, block)].reshape(block * 128, 128)
            k = tiles_k[pl.ds(b * block, block)].reshape(block * 128, 128)
            r = dot_nt(jnp.concatenate([d, k], axis=1), picked)
            for i in range(block):
                total = jnp.where(lane_s == b * block + i, r[i * 128 : (i + 1) * 128], total)
            return total

        product = lax.fori_loop(0, slots // block, products, jnp.zeros((128, slots), F32))
        hi, lo = halves(product)
        part = dot_nt(onehot_s[...], hi) + dot_nt(onehot_s[...], lo)
        part_s[it] = part.reshape(subs, nt, 128)
        for step in sorted(range(1, subs), key=lambda i: -ring_distance(i, subs)):
            send(part_s.at[it, to_x[step]], part_r.at[it, step - 1], 2 + it, (row, to_x[step]))
        if it == 0:
            arrived(gram_1.at[plane_view], 8)
            gram_2[in_line] = jnp.sum(gram_1[...], axis=0)
            for device in line_peers:
                send(gram_2.at[in_line], gram_2.at[in_line], 9, device)
        departed(window.at[it, pl.ds(0, 3 * subs - 1)], it)
        own = part_s[it, sub]
        arrived(part_r.at[it], 2 + it)
        coupled = own + part_r[it, 0]
        for step in range(2, subs):
            coupled = coupled + part_r[it, step - 1]
        image = shift * upper - mass * coupled
        image_s[...] = image

        def inner(b, total):
            for i in range(4):
                t = b * 4 + i
                piece = nat[:, pl.ds(pl.multiple_of(t * 128, 128), 128)]
                total = total + piece * jnp.broadcast_to(image_s[pl.ds(t, 1), :], piece.shape)
            return total

        parts_m[0:k0, :] = lax.fori_loop(0, nt // 4, inner, jnp.zeros((k0, 128), F32))
        if it > 0:
            parts_m[k0 : k0 + 1, :] = row_sum(column_s[...] * image)
        parts_m[63:64, :] = row_sum(image * image)
        pair_r[it, core] = row_sum(parts_m[...].T)
        send(pair_r.at[it, core], pair_r.at[it, core], 4 + it, at(0, 0, 1, 0))
        if it == 0:
            arrived(gram_2.at[line_view], 9)
            gram_3[in_plane] = jnp.sum(gram_2[...], axis=0)
            pl.semaphore_wait(ready_sem, plan.plane - 1)
        arrived(pair_r.at[it, 0], 4 + it)
        cube_r[it, in_cube] = pair_r[it, 0] + pair_r[it, 1]
        mine = cube_r.at[it, in_cube]
        for dz, dy, dx in plan.steps(plan.zs, plan.ys, subs):
            send(mine, mine, 6 + it, at(dz, dy, 0, dx))
        if it == 0:
            for _, device in plane_peers:
                send(gram_3.at[in_plane], gram_3.at[in_plane], 10, device)
        departed(part_r.at[it], 2 + it)
        departed(pair_r.at[it, 0], 4 + it)
        if it == 0:
            departed(gram_1.at[plane_view], 8)
            departed(gram_2.at[line_view], 9)
            departed(gram_3.at[plane_view], 10)
            arrived(gram_3.at[plane_view], 10)
            gram_m[...] = gram_3[...].reshape(64, 128) * scale
        gram = gram_m[...]
        turn = 2.0 * eye64 - gram
        up, low = upper_m[...], lower_m[...]
        lower_c = u1 + shift * u2
        arrived(cube_r.at[it, cube_view], 6 + it)
        sums = tree_sum([cube_r[it, i] for i in range(plan.cube)]) * scale

        own_square = lane_sum(jnp.where(lane == 63, sums, 0.0))
        first = jnp.where(lane < m, sums, 0.0)
        coef = jnp.broadcast_to(lane_sum(turn * first), (64, 128))
        coef_row = row_sum(eye64 * coef)
        gram_coef = row_sum(gram * coef)
        square = own_square + lane_sum(coef_row * (gram_coef - 2.0 * first))
        norm = jnp.sqrt(square + EPS)

        upper_c = jnp.where(row64 == m, norm, coef)
        weights = jnp.zeros((1, 128), F32)
        for _ in range(2):
            projection = row_sum(up * upper_c + low * lower_c)
            upper_c = upper_c - lane_sum(up * projection)
            lower_c = lower_c - lane_sum(low * projection)
            weights = weights + projection
        beta = jnp.sqrt(row_sum(upper_c * upper_c) + row_sum(lower_c * lower_c) + EPS)
        u1, u2 = upper_c / beta, lower_c / beta

        if it + 1 < ITERS:
            ratio = row_sum(jnp.where(row64 == m, u1, 0.0)) / norm
            coef_u[...] = u1 - ratio * coef
            coef_l[...] = u2
            held_u, lower = combined((coef_u, coef_l))
            upper = held_u + ratio * image
            pack(it + 1, upper, lower)
            exchange(it + 1)
            upper_m[...] = jnp.where(lane64 == cols, u1, up)
            lower_m[...] = jnp.where(lane64 == cols, u2, low)
        coef_u[...] = coef
        (taken,) = combined((coef_u,))
        column = (image - taken) / norm
        column_s[...] = column
        for t in range(nt):
            new_ref[it : it + 1, t * 128 : (t + 1) * 128] = column_s[t : t + 1, :]
        hess_ref[it : it + 1, :] = jnp.where(lane == cols, beta, weights)[:, 0 : j0 + ITERS]
        comp_ref[cols, 0:1, :] = row_sum(eye64 * u1)[:, 0 : k0 + ITERS]
        comp_ref[cols, 1:2, :] = row_sum(eye64 * u2)[:, 0 : k0 + ITERS]
        departed(cube_r.at[it, cube_view], 6 + it)
        if it + 1 < ITERS:
            held[m * nt : (m + 1) * nt, :] = column
            cross_row = (first - gram_coef) / norm
            cross_col = lane_sum(eye64 * cross_row)
            gram = jnp.where(row64 == m, cross_row, gram)
            gram = jnp.where(lane64 == m, cross_col, gram)
            gram = jnp.where((row64 == m) & (lane64 == m), square / (norm * norm), gram)
            gram_m[...] = gram


def put_out(*refs):
    ins, outs, sems = refs[:3], refs[3:6], refs[6]
    copies = [pltpu.make_async_copy(a, b, sems.at[i]) for i, (a, b) in enumerate(zip(ins, outs))]
    for copy in copies:
        copy.start()
    for copy in copies:
        copy.wait()


def on_device(stiffness, damping, tile_map, mass, shift, basis, compact, *, rows, subs):
    plan = Plan(rows, subs)
    k0, local = basis.shape
    j0 = compact.shape[2]
    slots = stiffness.shape[2]
    nt = local // 128
    unknowns = local * rows * subs
    chunk = 64 // plan.plane
    vmem = pl.BlockSpec(memory_space=pltpu.VMEM)
    hbm = pl.BlockSpec(memory_space=pltpu.HBM)
    smem = pl.BlockSpec(memory_space=pltpu.SMEM)
    scratch = [
        pltpu.VMEM((slots, 128, 128), BF16),
        pltpu.VMEM((slots, 128, 128), BF16),
        pltpu.VMEM((k0, local), F32),
        pltpu.VMEM((HELD * nt, 128), F32),
        pltpu.VMEM((2, slots), jnp.int32),
        pltpu.VMEM((nt, 128), F32),
        pltpu.VMEM((j0, 2, k0), F32),
        pltpu.VMEM((nt, 128), F32),
        pltpu.VMEM((nt, 128), F32),
        pltpu.VMEM((64, 128), F32),
        pltpu.VMEM((64, 128), F32),
        pltpu.VMEM((128, 128), F32),
        pltpu.VMEM((64, 128), F32),
        pltpu.VMEM((64, 128), F32),
        pltpu.VMEM((64, 128), F32),
        pltpu.VMEM((128, local // 8), BF16),
        pltpu.VMEM((slots, 3 * subs * nt), BF16),
        pltpu.VMEM((subs * nt, slots), BF16),
        pltpu.VMEM((ITERS, 3 * subs, nt, 256), BF16),
        pltpu.VMEM((ITERS, subs, nt, 128), F32),
        pltpu.VMEM((ITERS, subs - 1, nt, 128), F32),
        pltpu.VMEM((128, 128), F32),
        pltpu.VMEM((ITERS, 2, 1, 128), F32),
        pltpu.VMEM((ITERS, plan.cube, 1, 128), F32),
        pltpu.VMEM((plan.plane, chunk, 128), F32),
        pltpu.VMEM((plan.plane, chunk, 128), F32),
        pltpu.VMEM((plan.line, chunk, 128), F32),
        pltpu.VMEM((plan.plane, chunk, 128), F32),
        pltpu.SemaphoreType.DMA((6,)),
        pltpu.SemaphoreType.DMA((11,)),
        pltpu.SemaphoreType.DMA((11,)),
        pltpu.SemaphoreType.REGULAR,
    ]
    shapes = (
        jax.ShapeDtypeStruct((ITERS, local), F32),
        jax.ShapeDtypeStruct((j0 + ITERS, 2, k0 + ITERS), F32),
        jax.ShapeDtypeStruct((ITERS, j0 + ITERS), F32),
    )

    def pin(array):
        return pltpu.with_memory_space_constraint(array, pltpu.HBM)

    outs = pl.pallas_call(
        functools.partial(body, plan, k0, j0, unknowns, slots, nt),
        out_shape=shapes,
        in_specs=[hbm, hbm, hbm, hbm, smem, hbm, hbm],
        out_specs=(vmem, vmem, vmem),
        scratch_shapes=scratch,
        compiler_params=pltpu.CompilerParams(
            collective_id=0, has_side_effects=True, vmem_limit_bytes=48 << 20
        ),
        name="toar",
    )(
        pin(stiffness.reshape(stiffness.shape[2:])), pin(damping.reshape(damping.shape[2:])),
        pin(tile_map.reshape(2, slots)), pin(mass.reshape(nt, 128)), shift.reshape(1), pin(basis),
        pin(compact.transpose(2, 0, 1)),
    )
    new, comp, hess = pl.pallas_call(
        put_out,
        out_shape=shapes,
        in_specs=[vmem] * 3,
        out_specs=(hbm,) * 3,
        scratch_shapes=[pltpu.SemaphoreType.DMA((3,))],
        compiler_params=pltpu.CompilerParams(vmem_limit_bytes=2 << 20),
        name="put_out",
    )(*outs)
    return new, comp.transpose(1, 2, 0), hess.T


def solution(mesh):
    rows, subs = mesh.shape["rows"], mesh.shape["sub"]
    both = ("rows", "sub")
    return jax.shard_map(
        functools.partial(on_device, rows=rows, subs=subs),
        mesh=mesh,
        in_specs=(
            P("rows", "sub", None, None, None), P("rows", "sub", None, None, None),
            P("rows", "sub", None, None), P(both), P(), P(None, both), P(),
        ),
        out_specs=(P(None, both), P(), P()),
        check_vma=False,
    )
```

time: 70.4 us -> 59.3 us (0.84)
  local copies, waits for them, and re-layouts: 5.94 us -> 0 us
  Pallas kernels: 62.9 us -> 57.9 us
    pallas_call x1, Pallas kernels: 62.9 us -> 57.2 us  [on_device(): pl.pallas_call(functools.partial(body, plan, k0, j0, unknowns, slots, nt)...]
    unnamed x8 -> x0, local copies, waits for them, and re-layouts: 4.58 us -> none
    pallas_call x2 -> x0, local copies, waits for them, and re-layouts: 1.36 us -> none  [on_device(): pl.pallas_call(functools.partial(body, plan, k0, j0, unknowns, slots, nt)...]
where the time goes in v2:
time: 59.3 us; the launch traced here: 59.2 us
  Pallas kernels  57.9 us (98%)
  between operations  1.29 us (2%)
    pallas_call x1, Pallas kernels, on_device(): pl.pallas_call(functools.partial(body, plan, k0, j0, unknowns, slots, nt)...  57.2 us

profile of v2, /device:TPU:1, one launch (start us, length us, event | category | flops | bytes accessed | tf_op | source)
XLA Modules:
  0.0 59.2 jit_solution(15535582316848287431)
XLA Ops:
  1.3 57.2 %toar.1 = (f32[2,8192]{1,0:T(2,128)S(1)}, f32[59,2,60]{2,1,0:T(2,128)S(1)}, f32[2,59]{1,0:T(2,128)S(1)}) custom-call(bf16[128,128,128]{2,1,0:T(8,128)(2,1)} %bitcast.9, bf16[128,128,128]{2,1,0:T(8,128)(2,1)} %bitcast.10, s32[2,128]{1,0:T(2,128)} %bitcast.13, f32[64,128]{1,0:T(8,128)} %bitcast.12, f32[1]{0:T(128)} %bitcast.8.shift_ref, f32[58,8192]{1,0:T(8,128)} %basis_hbm.1, ...), custom_call_target="tpu_custom_call" | custom-call | tf_op jit(solution)/shard_map/toar/pallas_call | solution.py:438
  58.5 0.7 %put_out.1 = (f32[2,8192]{1,0:T(2,128)}, f32[59,2,60]{2,1,0:T(2,128)}, f32[2,59]{1,0:T(2,128)}) custom-call(f32[2,8192]{1,0:T(2,128)S(1)} %get-tuple-element.9.refs_0_, f32[59,2,60]{2,1,0:T(2,128)S(1)} %get-tuple-element.10.refs_1_, f32[2,59]{1,0:T(2,128)S(1)} %get-tuple-element.11.refs_2_), custom_call_target="tpu_custom_call" | custom-call | tf_op jit(solution)/shard_map/put_out/pallas_call | solution.py:453

commit v3 on v2

--- a/solution.py
+++ b/solution.py
@@ -67,7 +67,7 @@
     stiff_hbm, damp_hbm, map_hbm, mass_hbm, shift_ref, basis_hbm, compact_hbm,
     new_ref, comp_ref, hess_ref,
     tiles_d, tiles_k, nat, held, map_s, mass_s, compact_s, image_s, column_s, coef_u, coef_l,
-    square_s, upper_m, lower_m, gram_m, split_s, onehot_g, onehot_s, window, part_s, part_r,
+    square_s, upper_m, lower_m, gram_m, split_s, onehot_g, onehot_s, window_l, window_u, part_s, part_r,
     parts_m, pair_r, cube_r, gram_s, gram_1, gram_2, gram_3,
     copy_sem, send_sem, recv_sem, ready_sem,
 ):
@@ -135,20 +135,13 @@
     lane = iota((1, 128), 1)
     lane64 = iota((64, 128), 1)
     row64 = iota((64, 128), 0)
-    column_s[...] = jnp.zeros_like(column_s)
-    parts_m[...] = jnp.zeros_like(parts_m)
-    split_s[...] = jnp.zeros_like(split_s)
     held[k0 * nt :, :] = jnp.zeros((held.shape[0] - k0 * nt, 128), F32)
 
     small[0].wait()
-    for matrix, which in ((upper_m, 0), (lower_m, 1)):
-        square_s[...] = jnp.zeros_like(square_s)
-        square_s[0:j0, 0:k0] = compact_s[:, which, :]
-        matrix[...] = square_s[...].T[0:64]
-    comp_ref[...] = jnp.zeros_like(comp_ref)
-    comp_ref[0:j0, :, 0:k0] = compact_s[...]
-    u1 = jnp.broadcast_to(lane_sum(jnp.where(lane64 == j0 - 1, upper_m[...], 0.0)), (64, 128))
-    u2 = jnp.broadcast_to(lane_sum(jnp.where(lane64 == j0 - 1, lower_m[...], 0.0)), (64, 128))
+    last = compact_s[j0 - 1]
+    last = jnp.concatenate([last, jnp.zeros((2, 128 - k0), F32)], axis=1)
+    u1 = jnp.broadcast_to(lane_sum(eye64 * last[0:1]), (64, 128))
+    u2 = jnp.broadcast_to(lane_sum(eye64 * last[1:2]), (64, 128))
     coef_u[...] = u1
     coef_l[...] = u2
 
@@ -168,31 +161,31 @@
 
     lax.fori_loop(0, nt // 4, regroup, 0)
 
-    def combined(refs):
-        def add(b, totals):
+    def combined(ref):
+        def add(b, total):
             for i in range(4):
                 k = b * 4 + i
                 h = held[pl.ds(pl.multiple_of(k * nt, 8), nt), :]
-                totals = tuple(
-                    total + h * jnp.broadcast_to(ref[pl.ds(k, 1), :], h.shape)
-                    for total, ref in zip(totals, refs)
-                )
-            return totals
-        return lax.fori_loop(0, HELD // 4, add, tuple(jnp.zeros((nt, 128), F32) for _ in refs))
-
-    def pack(it, upper, lower):
-        window[it, subs + sub] = jnp.concatenate([upper, lower], axis=1).astype(BF16)
-
-    def exchange(it):
+                total = total + h * jnp.broadcast_to(ref[pl.ds(k, 1), :], h.shape)
+            return total
+        return lax.fori_loop(0, HELD // 4, add, jnp.zeros((nt, 128), F32))
+
+    def exchange(window, it, which, vector):
         mine = window.at[it, subs + sub]
+        mine[...] = vector.astype(BF16)
         for device in beside:
             place = sub if device[0] is below else 2 * subs + sub
-            send(mine, window.at[it, place], it, device)
-        for step in range(1, subs):
-            send(mine, mine, it, (row, to_x[step]))
-
-    upper, lower = combined((coef_u, coef_l))
-    pack(0, upper, lower)
+            send(mine, window.at[it, place], which, device)
+        for step in sorted(range(1, subs), key=lambda i: -ring_distance(i, subs)):
+            send(mine, mine, which, (row, to_x[step]))
+
+    lower = combined(coef_l)
+    pl.semaphore_wait(barrier, len(greeted))
+    exchange(window_l, 0, 0, lower)
+    upper = combined(coef_u)
+    exchange(window_u, 0, 1, upper)
+    for _, device in plane_peers:
+        pl.semaphore_signal(ready_sem, inc=1, device_id=device, device_id_type=MESH)
 
     wide = nat.shape[1] // 8
 
@@ -212,6 +205,20 @@
         for p in range(plan.plane):
             gram_s[p] = gram[p * chunk : (p + 1) * chunk]
         gram_1[in_plane] = gram_s[in_plane]
+
+    column_s[...] = jnp.zeros_like(column_s)
+    parts_m[...] = jnp.zeros_like(parts_m)
+    split_s[...] = jnp.zeros_like(split_s)
+    gram_ready()
+    for peer, device in plane_peers:
+        send(gram_s.at[peer], gram_1.at[in_plane], 10, device)
+
+    for matrix, which in ((upper_m, 0), (lower_m, 1)):
+        square_s[...] = jnp.zeros_like(square_s)
+        square_s[0:j0, 0:k0] = compact_s[:, which, :]
+        matrix[...] = square_s[...].T[0:64]
+    comp_ref[...] = jnp.zeros_like(comp_ref)
+    comp_ref[0:j0, :, 0:k0] = compact_s[...]
 
     small[1].wait()
     small[2].wait()
@@ -230,54 +237,55 @@
         & (spot >= first_tile) & (spot < last_tile)
     )
     onehot_g[...] = hit.astype(F32).astype(BF16)
-    gram_ready()
-
-    pl.semaphore_wait(barrier, len(greeted))
-    exchange(0)
-    for _, device in plane_peers:
-        pl.semaphore_signal(ready_sem, inc=1, device_id=device, device_id_type=MESH)
-    for peer, device in plane_peers:
-        send(gram_s.at[peer], gram_1.at[in_plane], 8, device)
 
     mass = mass_s[...]
     block = min(64, slots)
-    lane_s = iota((128, slots), 1)
+    pair_s = lax.div(iota((128, slots), 1), 2)
+    even_s = lax.rem(iota((slots, 128), 0), 2) == 0
+    others = pl.ds(0, 3 * subs - 1)
     plane_view = pl.ds(0, plan.plane - 1)
     line_view = pl.ds(0, plan.line - 1)
     cube_view = pl.ds(0, plan.cube - 1)
 
     for it in range(ITERS):
         m, cols = k0 + it, j0 + it
-        arrived(window.at[it, pl.ds(0, 3 * subs - 1)], it)
-        picked = jnp.dot(
-            onehot_g[...], window[it].reshape(3 * subs * nt, 256), preferred_element_type=F32
-        ).astype(BF16)
+        def products(tiles, window, which):
+            arrived(window.at[it, others], which)
+            source = window[it].reshape(3 * subs * nt, 128)
+            picked = jnp.dot(onehot_g[...], source, preferred_element_type=F32)
+            even = jnp.where(even_s, picked, 0.0)
+            picked = jnp.concatenate([even, picked - even], axis=1).astype(BF16)
+
+            def some(b, total):
+                t = tiles[pl.ds(b * block, block)].reshape(block // 2, 2, 128, 128)
+                pairs = jnp.concatenate([t[:, 0], t[:, 1]], axis=2).reshape(block * 64, 256)
+                r = dot_nt(pairs, picked)
+                for i in range(block // 2):
+                    here = pair_s == b * (block // 2) + i
+                    total = jnp.where(here, r[i * 128 : (i + 1) * 128], total)
+                return total
+
+            return lax.fori_loop(0, slots // block, some, jnp.zeros((128, slots), F32))
+
         if it == 0:
             for copy in tile_copies:
                 copy.wait()
-
-        def products(b, total):
-            d = tiles_d[pl.ds(b * block, block)].reshape(block * 128, 128)
-            k = tiles_k[pl.ds(b * block, block)].reshape(block * 128, 128)
-            r = dot_nt(jnp.concatenate([d, k], axis=1), picked)
-            for i in range(block):
-                total = jnp.where(lane_s == b * block + i, r[i * 128 : (i + 1) * 128], total)
-            return total
-
-        product = lax.fori_loop(0, slots // block, products, jnp.zeros((128, slots), F32))
+        product = products(tiles_k, window_l, 2 * it)
+        product = product + products(tiles_d, window_u, 2 * it + 1)
         hi, lo = halves(product)
         part = dot_nt(onehot_s[...], hi) + dot_nt(onehot_s[...], lo)
         part_s[it] = part.reshape(subs, nt, 128)
         for step in sorted(range(1, subs), key=lambda i: -ring_distance(i, subs)):
-            send(part_s.at[it, to_x[step]], part_r.at[it, step - 1], 2 + it, (row, to_x[step]))
+            send(part_s.at[it, to_x[step]], part_r.at[it, step - 1], 4 + it, (row, to_x[step]))
         if it == 0:
-            arrived(gram_1.at[plane_view], 8)
+            arrived(gram_1.at[plane_view], 10)
             gram_2[in_line] = jnp.sum(gram_1[...], axis=0)
             for device in line_peers:
-                send(gram_2.at[in_line], gram_2.at[in_line], 9, device)
-        departed(window.at[it, pl.ds(0, 3 * subs - 1)], it)
+                send(gram_2.at[in_line], gram_2.at[in_line], 11, device)
+        departed(window_l.at[it, others], 2 * it)
+        departed(window_u.at[it, others], 2 * it + 1)
         own = part_s[it, sub]
-        arrived(part_r.at[it], 2 + it)
+        arrived(part_r.at[it], 4 + it)
         coupled = own + part_r[it, 0]
         for step in range(2, subs):
             coupled = coupled + part_r[it, step - 1]
@@ -296,32 +304,32 @@
             parts_m[k0 : k0 + 1, :] = row_sum(column_s[...] * image)
         parts_m[63:64, :] = row_sum(image * image)
         pair_r[it, core] = row_sum(parts_m[...].T)
-        send(pair_r.at[it, core], pair_r.at[it, core], 4 + it, at(0, 0, 1, 0))
+        send(pair_r.at[it, core], pair_r.at[it, core], 6 + it, at(0, 0, 1, 0))
         if it == 0:
-            arrived(gram_2.at[line_view], 9)
+            arrived(gram_2.at[line_view], 11)
             gram_3[in_plane] = jnp.sum(gram_2[...], axis=0)
             pl.semaphore_wait(ready_sem, plan.plane - 1)
-        arrived(pair_r.at[it, 0], 4 + it)
+        arrived(pair_r.at[it, 0], 6 + it)
         cube_r[it, in_cube] = pair_r[it, 0] + pair_r[it, 1]
         mine = cube_r.at[it, in_cube]
         for dz, dy, dx in plan.steps(plan.zs, plan.ys, subs):
-            send(mine, mine, 6 + it, at(dz, dy, 0, dx))
+            send(mine, mine, 8 + it, at(dz, dy, 0, dx))
         if it == 0:
             for _, device in plane_peers:
-                send(gram_3.at[in_plane], gram_3.at[in_plane], 10, device)
-        departed(part_r.at[it], 2 + it)
-        departed(pair_r.at[it, 0], 4 + it)
+                send(gram_3.at[in_plane], gram_3.at[in_plane], 12, device)
+        departed(part_r.at[it], 4 + it)
+        departed(pair_r.at[it, 0], 6 + it)
         if it == 0:
-            departed(gram_1.at[plane_view], 8)
-            departed(gram_2.at[line_view], 9)
-            departed(gram_3.at[plane_view], 10)
-            arrived(gram_3.at[plane_view], 10)
+            departed(gram_1.at[plane_view], 10)
+            departed(gram_2.at[line_view], 11)
+            departed(gram_3.at[plane_view], 12)
+            arrived(gram_3.at[plane_view], 12)
             gram_m[...] = gram_3[...].reshape(64, 128) * scale
         gram = gram_m[...]
         turn = 2.0 * eye64 - gram
         up, low = upper_m[...], lower_m[...]
         lower_c = u1 + shift * u2
-        arrived(cube_r.at[it, cube_view], 6 + it)
+        arrived(cube_r.at[it, cube_view], 8 + it)
         sums = tree_sum([cube_r[it, i] for i in range(plan.cube)]) * scale
 
         own_square = lane_sum(jnp.where(lane == 63, sums, 0.0))
@@ -346,22 +354,20 @@
             ratio = row_sum(jnp.where(row64 == m, u1, 0.0)) / norm
             coef_u[...] = u1 - ratio * coef
             coef_l[...] = u2
-            held_u, lower = combined((coef_u, coef_l))
-            upper = held_u + ratio * image
-            pack(it + 1, upper, lower)
-            exchange(it + 1)
+            exchange(window_l, it + 1, 2 * it + 2, combined(coef_l))
+            upper = combined(coef_u) + ratio * image
+            exchange(window_u, it + 1, 2 * it + 3, upper)
             upper_m[...] = jnp.where(lane64 == cols, u1, up)
             lower_m[...] = jnp.where(lane64 == cols, u2, low)
         coef_u[...] = coef
-        (taken,) = combined((coef_u,))
-        column = (image - taken) / norm
+        column = (image - combined(coef_u)) / norm
         column_s[...] = column
         for t in range(nt):
             new_ref[it : it + 1, t * 128 : (t + 1) * 128] = column_s[t : t + 1, :]
         hess_ref[it : it + 1, :] = jnp.where(lane == cols, beta, weights)[:, 0 : j0 + ITERS]
         comp_ref[cols, 0:1, :] = row_sum(eye64 * u1)[:, 0 : k0 + ITERS]
         comp_ref[cols, 1:2, :] = row_sum(eye64 * u2)[:, 0 : k0 + ITERS]
-        departed(cube_r.at[it, cube_view], 6 + it)
+        departed(cube_r.at[it, cube_view], 8 + it)
         if it + 1 < ITERS:
             held[m * nt : (m + 1) * nt, :] = column
             cross_row = (first - gram_coef) / norm
@@ -411,7 +417,8 @@
         pltpu.VMEM((128, local // 8), BF16),
         pltpu.VMEM((slots, 3 * subs * nt), BF16),
         pltpu.VMEM((subs * nt, slots), BF16),
-        pltpu.VMEM((ITERS, 3 * subs, nt, 256), BF16),
+        pltpu.VMEM((ITERS, 3 * subs, nt, 128), BF16),
+        pltpu.VMEM((ITERS, 3 * subs, nt, 128), BF16),
         pltpu.VMEM((ITERS, subs, nt, 128), F32),
         pltpu.VMEM((ITERS, subs - 1, nt, 128), F32),
         pltpu.VMEM((128, 128), F32),
@@ -422,8 +429,8 @@
         pltpu.VMEM((plan.line, chunk, 128), F32),
         pltpu.VMEM((plan.plane, chunk, 128), F32),
         pltpu.SemaphoreType.DMA((6,)),
-        pltpu.SemaphoreType.DMA((11,)),
-        pltpu.SemaphoreType.DMA((11,)),
+        pltpu.SemaphoreType.DMA((13,)),
+        pltpu.SemaphoreType.DMA((13,)),
         pltpu.SemaphoreType.REGULAR,
     ]
     shapes = (

time: 59.3 us -> 55.8 us (0.941)
  Pallas kernels: 57.9 us -> 54.4 us
    pallas_call x1, Pallas kernels: 57.2 us -> 53.7 us  [on_device(): pl.pallas_call(functools.partial(body, plan, k0, j0, unknowns, slots, nt)...]
where the time goes in v3:
time: 55.8 us; the launch traced here: 55.7 us
  Pallas kernels  54.4 us (97%)
  between operations  1.29 us (2%)
    pallas_call x1, Pallas kernels, on_device(): pl.pallas_call(functools.partial(body, plan, k0, j0, unknowns, slots, nt)...  53.7 us

profile of v3, /device:TPU:1, one launch (start us, length us, event | category | flops | bytes accessed | tf_op | source)
XLA Modules:
  0.0 55.7 jit_solution(14793453277226571825)
XLA Ops:
  1.3 53.7 %toar.1 = (f32[2,8192]{1,0:T(2,128)S(1)}, f32[59,2,60]{2,1,0:T(2,128)S(1)}, f32[2,59]{1,0:T(2,128)S(1)}) custom-call(bf16[128,128,128]{2,1,0:T(8,128)(2,1)} %bitcast.9, bf16[128,128,128]{2,1,0:T(8,128)(2,1)} %bitcast.10, s32[2,128]{1,0:T(2,128)} %bitcast.13, f32[64,128]{1,0:T(8,128)} %bitcast.12, f32[1]{0:T(128)} %bitcast.8.shift_ref, f32[58,8192]{1,0:T(8,128)} %basis_hbm.1, ...), custom_call_target="tpu_custom_call" | custom-call | tf_op jit(solution)/shard_map/toar/pallas_call | solution.py:445
  55.0 0.7 %put_out.1 = (f32[2,8192]{1,0:T(2,128)}, f32[59,2,60]{2,1,0:T(2,128)}, f32[2,59]{1,0:T(2,128)}) custom-call(f32[2,8192]{1,0:T(2,128)S(1)} %get-tuple-element.9.refs_0_, f32[59,2,60]{2,1,0:T(2,128)S(1)} %get-tuple-element.10.refs_1_, f32[2,59]{1,0:T(2,128)S(1)} %get-tuple-element.11.refs_2_), custom_call_target="tpu_custom_call" | custom-call | tf_op jit(solution)/shard_map/put_out/pallas_call | solution.py:460

commit v4 on v3

--- a/solution.py
+++ b/solution.py
@@ -67,7 +67,7 @@
     stiff_hbm, damp_hbm, map_hbm, mass_hbm, shift_ref, basis_hbm, compact_hbm,
     new_ref, comp_ref, hess_ref,
     tiles_d, tiles_k, nat, held, map_s, mass_s, compact_s, image_s, column_s, coef_u, coef_l,
-    square_s, upper_m, lower_m, gram_m, split_s, onehot_g, onehot_s, window_l, window_u, part_s, part_r,
+    square_s, upper_m, lower_m, gram_m, split_s, onehot_g, onehot_s, window_l, window_u, part_f, part_s, part_r,
     parts_m, pair_r, cube_r, gram_s, gram_1, gram_2, gram_3,
     copy_sem, send_sem, recv_sem, ready_sem,
 ):
@@ -163,12 +163,12 @@
 
     def combined(ref):
         def add(b, total):
-            for i in range(4):
-                k = b * 4 + i
+            for i in range(12):
+                k = b * 12 + i
                 h = held[pl.ds(pl.multiple_of(k * nt, 8), nt), :]
                 total = total + h * jnp.broadcast_to(ref[pl.ds(k, 1), :], h.shape)
             return total
-        return lax.fori_loop(0, HELD // 4, add, jnp.zeros((nt, 128), F32))
+        return lax.fori_loop(0, HELD // 12, add, jnp.zeros((nt, 128), F32))
 
     def exchange(window, it, which, vector):
         mine = window.at[it, subs + sub]
@@ -274,7 +274,8 @@
         product = product + products(tiles_d, window_u, 2 * it + 1)
         hi, lo = halves(product)
         part = dot_nt(onehot_s[...], hi) + dot_nt(onehot_s[...], lo)
-        part_s[it] = part.reshape(subs, nt, 128)
+        part_f[...] = part.reshape(subs, nt, 128)
+        part_s[it] = part.reshape(subs, nt, 128).astype(BF16)
         for step in sorted(range(1, subs), key=lambda i: -ring_distance(i, subs)):
             send(part_s.at[it, to_x[step]], part_r.at[it, step - 1], 4 + it, (row, to_x[step]))
         if it == 0:
@@ -284,22 +285,22 @@
                 send(gram_2.at[in_line], gram_2.at[in_line], 11, device)
         departed(window_l.at[it, others], 2 * it)
         departed(window_u.at[it, others], 2 * it + 1)
-        own = part_s[it, sub]
+        own = part_f[sub]
         arrived(part_r.at[it], 4 + it)
-        coupled = own + part_r[it, 0]
-        for step in range(2, subs):
-            coupled = coupled + part_r[it, step - 1]
+        coupled = own
+        for step in range(1, subs):
+            coupled = coupled + part_r[it, step - 1].astype(F32)
         image = shift * upper - mass * coupled
         image_s[...] = image
 
         def inner(b, total):
-            for i in range(4):
-                t = b * 4 + i
+            for i in range(8):
+                t = b * 8 + i
                 piece = nat[:, pl.ds(pl.multiple_of(t * 128, 128), 128)]
                 total = total + piece * jnp.broadcast_to(image_s[pl.ds(t, 1), :], piece.shape)
             return total
 
-        parts_m[0:k0, :] = lax.fori_loop(0, nt // 4, inner, jnp.zeros((k0, 128), F32))
+        parts_m[0:k0, :] = lax.fori_loop(0, nt // 8, inner, jnp.zeros((k0, 128), F32))
         if it > 0:
             parts_m[k0 : k0 + 1, :] = row_sum(column_s[...] * image)
         parts_m[63:64, :] = row_sum(image * image)
@@ -419,8 +420,9 @@
         pltpu.VMEM((subs * nt, slots), BF16),
         pltpu.VMEM((ITERS, 3 * subs, nt, 128), BF16),
         pltpu.VMEM((ITERS, 3 * subs, nt, 128), BF16),
-        pltpu.VMEM((ITERS, subs, nt, 128), F32),
-        pltpu.VMEM((ITERS, subs - 1, nt, 128), F32),
+        pltpu.VMEM((subs, nt, 128), F32),
+        pltpu.VMEM((ITERS, subs, nt, 128), BF16),
+        pltpu.VMEM((ITERS, subs - 1, nt, 128), BF16),
         pltpu.VMEM((128, 128), F32),
         pltpu.VMEM((ITERS, 2, 1, 128), F32),
         pltpu.VMEM((ITERS, plan.cube, 1, 128), F32),

time: 55.8 us -> 54.9 us (0.984)
  Pallas kernels: 54.4 us -> 53.5 us
    pallas_call x1, Pallas kernels: 53.7 us -> 52.8 us  [on_device(): pl.pallas_call(functools.partial(body, plan, k0, j0, unknowns, slots, nt)...]
where the time goes in v4:
time: 54.9 us; the launch traced here: 54.8 us
  Pallas kernels  53.5 us (97%)
  between operations  1.29 us (2%)
    pallas_call x1, Pallas kernels, on_device(): pl.pallas_call(functools.partial(body, plan, k0, j0, unknowns, slots, nt)...  52.8 us

profile of v4, /device:TPU:1, one launch (start us, length us, event | category | flops | bytes accessed | tf_op | source)
XLA Modules:
  0.0 54.8 jit_solution(15390986641340532668)
XLA Ops:
  1.3 52.8 %toar.1 = (f32[2,8192]{1,0:T(2,128)S(1)}, f32[59,2,60]{2,1,0:T(2,128)S(1)}, f32[2,59]{1,0:T(2,128)S(1)}) custom-call(bf16[128,128,128]{2,1,0:T(8,128)(2,1)} %bitcast.9, bf16[128,128,128]{2,1,0:T(8,128)(2,1)} %bitcast.10, s32[2,128]{1,0:T(2,128)} %bitcast.13, f32[64,128]{1,0:T(8,128)} %bitcast.12, f32[1]{0:T(128)} %bitcast.8.shift_ref, f32[58,8192]{1,0:T(8,128)} %basis_hbm.1, ...), custom_call_target="tpu_custom_call" | custom-call | tf_op jit(solution)/shard_map/toar/pallas_call | solution.py:447
  54.1 0.7 %put_out.1 = (f32[2,8192]{1,0:T(2,128)}, f32[59,2,60]{2,1,0:T(2,128)}, f32[2,59]{1,0:T(2,128)}) custom-call(f32[2,8192]{1,0:T(2,128)S(1)} %get-tuple-element.9.refs_0_, f32[59,2,60]{2,1,0:T(2,128)S(1)} %get-tuple-element.10.refs_1_, f32[2,59]{1,0:T(2,128)S(1)} %get-tuple-element.11.refs_2_), custom_call_target="tpu_custom_call" | custom-call | tf_op jit(solution)/shard_map/put_out/pallas_call | solution.py:462

commit v5 on v4

--- a/solution.py
+++ b/solution.py
@@ -98,14 +98,14 @@
         (to_y[dy] * subs + to_x[dx], at(0, dy, 0, dx)) for dy, dx in plan.steps(plan.ys, subs)
     ]
     line_peers = [at(dz, 0, dc, 0) for dz, dc in plan.steps(plan.zs, plan.cores)]
-    beside = [
-        (device, to_x[dx])
-        for dx in sorted(range(subs), key=lambda i: -ring_distance(i, subs))
-        for device in (above, below)
-    ]
+    partner = row + 1 - 2 * core
+    across = jnp.where(core == 0, above, below)
+    to_partner = jnp.where(core == 0, 0, 2 * subs)
+    to_across = 2 * subs - to_partner
+    far_first = sorted(range(subs), key=lambda i: -ring_distance(i, subs))
 
     barrier = pltpu.get_barrier_semaphore()
-    greeted = line_peers + beside + [device for _, device in plane_peers]
+    greeted = line_peers + [(across, x) for x in to_x] + [device for _, device in plane_peers]
     for device in greeted:
         pl.semaphore_signal(barrier, inc=1, device_id=device, device_id_type=MESH)
 
@@ -173,11 +173,17 @@
     def exchange(window, it, which, vector):
         mine = window.at[it, subs + sub]
         mine[...] = vector.astype(BF16)
-        for device in beside:
-            place = sub if device[0] is below else 2 * subs + sub
-            send(mine, window.at[it, place], which, device)
-        for step in sorted(range(1, subs), key=lambda i: -ring_distance(i, subs)):
+        for step in far_first[:-1]:
             send(mine, mine, which, (row, to_x[step]))
+        for step in far_first:
+            send(mine, window.at[it, to_across + sub], which + 4, (across, to_x[step]))
+        send(mine, window.at[it, to_partner + sub], which + 4, (partner, sub))
+
+    def relay(window, it, which):
+        arrived(window.at[it, pl.ds(0, subs - 1)], which)
+        for step in far_first[:-1]:
+            theirs = window.at[it, subs + to_x[step]]
+            send(theirs, window.at[it, to_partner + to_x[step]], which + 4, (partner, sub))
 
     lower = combined(coef_l)
     pl.semaphore_wait(barrier, len(greeted))
@@ -211,7 +217,7 @@
     split_s[...] = jnp.zeros_like(split_s)
     gram_ready()
     for peer, device in plane_peers:
-        send(gram_s.at[peer], gram_1.at[in_plane], 10, device)
+        send(gram_s.at[peer], gram_1.at[in_plane], 14, device)
 
     for matrix, which in ((upper_m, 0), (lower_m, 1)):
         square_s[...] = jnp.zeros_like(square_s)
@@ -242,7 +248,8 @@
     block = min(64, slots)
     pair_s = lax.div(iota((128, slots), 1), 2)
     even_s = lax.rem(iota((slots, 128), 0), 2) == 0
-    others = pl.ds(0, 3 * subs - 1)
+    others = pl.ds(0, 2 * subs)
+    peers = pl.ds(0, subs - 1)
     plane_view = pl.ds(0, plan.plane - 1)
     line_view = pl.ds(0, plan.line - 1)
     cube_view = pl.ds(0, plan.cube - 1)
@@ -250,7 +257,7 @@
     for it in range(ITERS):
         m, cols = k0 + it, j0 + it
         def products(tiles, window, which):
-            arrived(window.at[it, others], which)
+            arrived(window.at[it, others], which + 4)
             source = window[it].reshape(3 * subs * nt, 128)
             picked = jnp.dot(onehot_g[...], source, preferred_element_type=F32)
             even = jnp.where(even_s, picked, 0.0)
@@ -267,6 +274,8 @@
 
             return lax.fori_loop(0, slots // block, some, jnp.zeros((128, slots), F32))
 
+        relay(window_l, it, 2 * it)
+        relay(window_u, it, 2 * it + 1)
         if it == 0:
             for copy in tile_copies:
                 copy.wait()
@@ -277,16 +286,17 @@
         part_f[...] = part.reshape(subs, nt, 128)
         part_s[it] = part.reshape(subs, nt, 128).astype(BF16)
         for step in sorted(range(1, subs), key=lambda i: -ring_distance(i, subs)):
-            send(part_s.at[it, to_x[step]], part_r.at[it, step - 1], 4 + it, (row, to_x[step]))
+            send(part_s.at[it, to_x[step]], part_r.at[it, step - 1], 8 + it, (row, to_x[step]))
         if it == 0:
-            arrived(gram_1.at[plane_view], 10)
+            arrived(gram_1.at[plane_view], 14)
             gram_2[in_line] = jnp.sum(gram_1[...], axis=0)
             for device in line_peers:
-                send(gram_2.at[in_line], gram_2.at[in_line], 11, device)
-        departed(window_l.at[it, others], 2 * it)
-        departed(window_u.at[it, others], 2 * it + 1)
+                send(gram_2.at[in_line], gram_2.at[in_line], 15, device)
+        for which, window in ((2 * it, window_l), (2 * it + 1, window_u)):
+            departed(window.at[it, peers], which)
+            departed(window.at[it, others], which + 4)
         own = part_f[sub]
-        arrived(part_r.at[it], 4 + it)
+        arrived(part_r.at[it], 8 + it)
         coupled = own
         for step in range(1, subs):
             coupled = coupled + part_r[it, step - 1].astype(F32)
@@ -305,32 +315,32 @@
             parts_m[k0 : k0 + 1, :] = row_sum(column_s[...] * image)
         parts_m[63:64, :] = row_sum(image * image)
         pair_r[it, core] = row_sum(parts_m[...].T)
-        send(pair_r.at[it, core], pair_r.at[it, core], 6 + it, at(0, 0, 1, 0))
+        send(pair_r.at[it, core], pair_r.at[it, core], 10 + it, at(0, 0, 1, 0))
         if it == 0:
-            arrived(gram_2.at[line_view], 11)
+            arrived(gram_2.at[line_view], 15)
             gram_3[in_plane] = jnp.sum(gram_2[...], axis=0)
             pl.semaphore_wait(ready_sem, plan.plane - 1)
-        arrived(pair_r.at[it, 0], 6 + it)
+        arrived(pair_r.at[it, 0], 10 + it)
         cube_r[it, in_cube] = pair_r[it, 0] + pair_r[it, 1]
         mine = cube_r.at[it, in_cube]
         for dz, dy, dx in plan.steps(plan.zs, plan.ys, subs):
-            send(mine, mine, 8 + it, at(dz, dy, 0, dx))
+            send(mine, mine, 12 + it, at(dz, dy, 0, dx))
         if it == 0:
             for _, device in plane_peers:
-                send(gram_3.at[in_plane], gram_3.at[in_plane], 12, device)
-        departed(part_r.at[it], 4 + it)
-        departed(pair_r.at[it, 0], 6 + it)
+                send(gram_3.at[in_plane], gram_3.at[in_plane], 16, device)
+        departed(part_r.at[it], 8 + it)
+        departed(pair_r.at[it, 0], 10 + it)
         if it == 0:
-            departed(gram_1.at[plane_view], 10)
-            departed(gram_2.at[line_view], 11)
-            departed(gram_3.at[plane_view], 12)
-            arrived(gram_3.at[plane_view], 12)
+            departed(gram_1.at[plane_view], 14)
+            departed(gram_2.at[line_view], 15)
+            departed(gram_3.at[plane_view], 16)
+            arrived(gram_3.at[plane_view], 16)
             gram_m[...] = gram_3[...].reshape(64, 128) * scale
         gram = gram_m[...]
         turn = 2.0 * eye64 - gram
         up, low = upper_m[...], lower_m[...]
         lower_c = u1 + shift * u2
-        arrived(cube_r.at[it, cube_view], 8 + it)
+        arrived(cube_r.at[it, cube_view], 12 + it)
         sums = tree_sum([cube_r[it, i] for i in range(plan.cube)]) * scale
 
         own_square = lane_sum(jnp.where(lane == 63, sums, 0.0))
@@ -368,7 +378,7 @@
         hess_ref[it : it + 1, :] = jnp.where(lane == cols, beta, weights)[:, 0 : j0 + ITERS]
         comp_ref[cols, 0:1, :] = row_sum(eye64 * u1)[:, 0 : k0 + ITERS]
         comp_ref[cols, 1:2, :] = row_sum(eye64 * u2)[:, 0 : k0 + ITERS]
-        departed(cube_r.at[it, cube_view], 8 + it)
+        departed(cube_r.at[it, cube_view], 12 + it)
         if it + 1 < ITERS:
             held[m * nt : (m + 1) * nt, :] = column
             cross_row = (first - gram_coef) / norm
@@ -431,8 +441,8 @@
         pltpu.VMEM((plan.line, chunk, 128), F32),
         pltpu.VMEM((plan.plane, chunk, 128), F32),
         pltpu.SemaphoreType.DMA((6,)),
-        pltpu.SemaphoreType.DMA((13,)),
-        pltpu.SemaphoreType.DMA((13,)),
+        pltpu.SemaphoreType.DMA((17,)),
+        pltpu.SemaphoreType.DMA((17,)),
         pltpu.SemaphoreType.REGULAR,
     ]
     shapes = (

time: 54.9 us -> 54.5 us (level)
  no operation moved by 1% of the time
where the time goes in v5:
time: 54.5 us; the launch traced here: 54.4 us
  Pallas kernels  53.1 us (97%)
  between operations  1.29 us (2%)
    pallas_call x1, Pallas kernels, on_device(): pl.pallas_call(functools.partial(body, plan, k0, j0, unknowns, slots, nt)...  52.4 us

profile of v5, /device:TPU:1, one launch (start us, length us, event | category | flops | bytes accessed | tf_op | source)
XLA Modules:
  0.0 54.4 jit_solution(10006049352713718313)
XLA Ops:
  1.3 52.4 %toar.1 = (f32[2,8192]{1,0:T(2,128)S(1)}, f32[59,2,60]{2,1,0:T(2,128)S(1)}, f32[2,59]{1,0:T(2,128)S(1)}) custom-call(bf16[128,128,128]{2,1,0:T(8,128)(2,1)} %bitcast.9, bf16[128,128,128]{2,1,0:T(8,128)(2,1)} %bitcast.10, s32[2,128]{1,0:T(2,128)} %bitcast.13, f32[64,128]{1,0:T(8,128)} %bitcast.12, f32[1]{0:T(128)} %bitcast.8.shift_ref, f32[58,8192]{1,0:T(8,128)} %basis_hbm.1, ...), custom_call_target="tpu_custom_call" | custom-call | tf_op jit(solution)/shard_map/toar/pallas_call | solution.py:457
  53.7 0.7 %put_out.1 = (f32[2,8192]{1,0:T(2,128)}, f32[59,2,60]{2,1,0:T(2,128)}, f32[2,59]{1,0:T(2,128)}) custom-call(f32[2,8192]{1,0:T(2,128)S(1)} %get-tuple-element.9.refs_0_, f32[59,2,60]{2,1,0:T(2,128)S(1)} %get-tuple-element.10.refs_1_, f32[2,59]{1,0:T(2,128)S(1)} %get-tuple-element.11.refs_2_), custom_call_target="tpu_custom_call" | custom-call | tf_op jit(solution)/shard_map/put_out/pallas_call | solution.py:472
